TPU v7x, 256 devices: a whole 4x4x8 slice. The times are simulated.
256 devices in a mesh: fsdp: 32 (over z_hi, x, core), tp: 8 (over y, z_lo).
Axes of the slice: x: 4, y: 4, z: 8 (z_hi: 4, z_lo: 2; z = z_hi * 2 + z_lo), core: 2. Of those that a mesh axis runs over, the one named last changes fastest.
Arguments:
- hidden: bfloat16 [8192, 8192], P('fsdp'), may hold values from -6 to 6
- norm_gain: float32 [8192], replicated, may hold values from 0.6 to 6, as said below
- w_query: bfloat16 [8192, 4096], P('fsdp', 'tp'), may hold values from -0.09375 to 0.09375
- w_key: bfloat16 [8192, 512], P('fsdp'), may hold values from -0.09375 to 0.09375
- w_value: bfloat16 [8192, 512], P('fsdp'), may hold values from -0.0625 to 0.0625
- bias_query: bfloat16 [4096], P('tp'), may hold values from -3 to 3
- bias_key: bfloat16 [512], replicated, may hold values from -3 to 3
- bias_value: bfloat16 [512], replicated, may hold values from -3 to 3
- w_out: bfloat16 [4096, 8192], P('tp', 'fsdp'), may hold values from -0.09375 to 0.09375
- seq_lengths: int32 [4], replicated, may hold values from 1 to 6144, 8192 in all
Outputs:
- hidden_out: float32 [8192, 8192], P(('fsdp', 'tp'))
Inputs may be any that keep to these rules, and one draw needn't show every extreme that they name: `seq_lengths`: 4 sequences packed in order; the lengths sum to 8192 and the longest has exactly 6144 tokens. `norm_gain`: positive gains.
All inputs are finite; a program needn't handle non-finite values.
Results may differ from a plain program's by a relative error of at most 0.014.
The roundings to bfloat16 on the way count: a program that leaves them out, or rounds other values in their place, can miss the bound.
Values may be sent and summed in bfloat16 or wider, within the bound.
No kernel may reach another device: no remote copies, remote signals or barrier semaphores. Data moves between devices by JAX's collectives and lax.ppermute only.
A program may use at most 128 MiB of HBM per device.

v0:
```python
import functools
import math

import jax
import jax.numpy as jnp
from jax import lax
from jax.experimental import pallas as pl
from jax.experimental.pallas import tpu as pltpu
from jax.sharding import Mesh
from jax.sharding import PartitionSpec as P


HEAD = 128
ROPE_BASE = 1000000.0
EPSILON = 1e-06
FLOOR = -1e30
FSDP = ("zh", "x", "co")
TP = ("y", "zl")
ALL = FSDP + TP
BF16 = jnp.bfloat16
F32 = jnp.float32
OFFSETS = (0, -1, 1, 2)


def vmem(count):
    return [pl.BlockSpec(memory_space=pltpu.VMEM)] * count


def smem(count):
    return [pl.BlockSpec(memory_space=pltpu.SMEM)] * count


def call(body, out_shape, ins, scratch=(), smem_count=0, extra=0, flops=0, moved=0, transcendentals=0):
    return pl.pallas_call(
        body,
        out_shape=out_shape,
        in_specs=smem(smem_count) + vmem(len(ins) - smem_count),
        out_specs=pl.BlockSpec(memory_space=pltpu.VMEM),
        scratch_shapes=list(scratch),
        compiler_params=pltpu.CompilerParams(
            vmem_limit_bytes=sum(math.prod(a.shape) * a.dtype.itemsize for a in [*ins, out_shape])
            + extra
            + (4 << 20)
        ),
        cost_estimate=pl.CostEstimate(
            flops=flops, bytes_accessed=moved, transcendentals=transcendentals
        ),
    )(*ins)


def shift(array, axis, by):
    return lax.ppermute(array, axis, [(i, (i + by) % 4) for i in range(4)])


def swap(array, axis):
    return lax.ppermute(array, axis, [(0, 1), (1, 0)])


def around(array, axis):
    return shift(array, axis, 1), shift(array, axis, -1)


def spread(array, axes, count):
    copies = jnp.broadcast_to(array[None], (count,) + array.shape)
    return lax.all_to_all(copies, axes, 0, 0, tiled=True)


def halves(before, after, axis):
    half = before.shape[0] // 2
    return jnp.concatenate([shift(before[:half], axis, 1), shift(after[half:], axis, -1)])


def both_cores(near):
    far = [swap(a, "co") for a in near]
    return [(0, x, 0, a) for x, a in enumerate(near)] + [(1, x, 0, a) for x, a in enumerate(far)]


def ring_gather(array, axis):
    before, after = around(array, axis)
    return [array, before, after, halves(before, after, axis)]


def normalize(hidden_ref, gain_ref, out_ref):
    rows, width = hidden_ref.shape
    span = 256
    chunk = 32

    def step(i, carry):
        at = pl.ds(pl.multiple_of(i * chunk, chunk), chunk)
        total = jnp.zeros((chunk, span), F32)
        for k in range(width // span):
            part = hidden_ref[at, k * span : (k + 1) * span].astype(F32)
            total = total + part * part
        scale = lax.rsqrt(jnp.sum(total, axis=1, keepdims=True) / width + EPSILON)
        for k in range(width // span):
            cols = slice(k * span, (k + 1) * span)
            part = hidden_ref[at, cols].astype(F32)
            out_ref[at, cols] = (part * scale * gain_ref[:, cols]).astype(BF16)
        return carry

    lax.fori_loop(0, rows // chunk, step, 0)


def turn_heads(total, bias_ref, cos_ref, sin_ref, out_ref):
    for h in range(out_ref.shape[1] // HEAD):
        at = slice(h * HEAD, (h + 1) * HEAD)
        u = total[:, at] + bias_ref[:, at]
        out_ref[:, at] = (u * cos_ref[...] + pltpu.roll(u, HEAD // 2, 1) * sin_ref[...]).astype(BF16)


def project_kernel(places, order_ref, hidden_ref, gain_ref, bias_ref, cos_ref, sin_ref, *refs):
    pieces, out_ref, normed_ref = refs[:-2], refs[-2], refs[-1]
    normalize(hidden_ref, gain_ref, normed_ref)
    total = None
    group = 4
    for (core, x, z), piece in zip(places, pieces):
        count, rows, cols = piece.shape
        for k in range(0, count, group):
            taken = [order_ref[(core * 4 + x) * 4 + z + k + i] for i in range(group)]
            part = jnp.dot(
                jnp.concatenate(
                    [normed_ref[:, pl.ds(pl.multiple_of(t * rows, rows), rows)] for t in taken], axis=1
                ),
                piece[k : k + group].reshape(group * rows, cols),
                preferred_element_type=F32,
            )
            total = part if total is None else total + part
    turn_heads(total, bias_ref, cos_ref, sin_ref, out_ref)


def attend_kernel(places, block_ref, info_ref, query_ref, begin_ref, *refs):
    pieces = refs[: len(places)]
    out_ref, key_ref, value_ref, slot_ref, score_ref, top_ref, sum_ref, mix_ref = refs[len(places) :]
    rows, cols = query_ref.shape
    heads = cols // HEAD
    span = pieces[0].shape[1]
    mine, lowest, full_from = info_ref[0], info_ref[1], info_ref[2]
    last = key_ref.shape[0] - 1
    rate = HEAD**-0.5 * math.log2(math.e)

    def take(slot, number, block):
        key_ref[slot] = block[:, :HEAD]
        value_ref[slot] = block[:, HEAD:].T
        slot_ref[slot] = number

    counts = (jnp.int32(0), jnp.int32(0))
    for (core, x, z), piece in zip(places, pieces):

        def sort(k, counts, piece=piece, base=(core * 4 + x) * 4 + z):
            plain, masked = counts
            number = block_ref[base + k]
            needed = (number <= mine) & (number >= lowest)
            is_plain = needed & (number < mine) & (number >= full_from)
            slot = jnp.where(is_plain, plain, last - masked)
            pl.when(needed)(functools.partial(take, slot, number, piece.at[k]))
            return (
                plain + is_plain.astype(jnp.int32),
                masked + (needed & jnp.logical_not(is_plain)).astype(jnp.int32),
            )

        counts = lax.fori_loop(0, piece.shape[0], sort, counts)
    plain, masked = counts
    odd = plain % 2

    @pl.when(odd == 1)
    def _():
        key_ref[last - masked] = key_ref[plain - 1]
        value_ref[last - masked] = value_ref[plain - 1]
        slot_ref[last - masked] = slot_ref[plain - 1]

    plain, masked = plain - odd, masked + odd

    @pl.when(masked % 2 == 1)
    def _():
        take(last - masked, jnp.int32(1 << 20), pieces[0].at[0])

    top_ref[...] = jnp.full(top_ref.shape, FLOOR, F32)
    sum_ref[...] = jnp.zeros(sum_ref.shape, F32)
    mix_ref[...] = jnp.zeros(mix_ref.shape, F32)

    def fold(slots, allowed):
        def score(h):
            for i, slot in enumerate(slots):
                score_ref[h % 2, i * span : (i + 1) * span] = lax.dot_general(
                    key_ref[slot],
                    query_ref[:, h * HEAD : (h + 1) * HEAD],
                    (((1,), (1,)), ((), ())),
                    preferred_element_type=F32,
                )

        score(0)
        for h in range(heads):
            if h + 1 < heads:
                score(h + 1)
            at = slice(h * rows, (h + 1) * rows)
            scores = score_ref[h % 2]
            if allowed is not None:
                scores = jnp.where(allowed, scores, FLOOR)
            old = top_ref[:, at]
            new = jnp.maximum(old, jnp.max(scores, axis=0, keepdims=True))
            weights = jnp.exp2((scores - new) * rate)
            factor = jnp.exp2((old - new) * rate)
            top_ref[:, at] = new
            sum_ref[:, at] = sum_ref[:, at] * factor + jnp.sum(weights, axis=0, keepdims=True)
            mix_ref[:, at] = mix_ref[:, at] * factor + jnp.dot(
                jnp.concatenate([value_ref[slot] for slot in slots], axis=1),
                weights.astype(BF16),
                preferred_element_type=F32,
            )

    def masked_step(i, carry):
        slots = (last - 2 * i, last - 2 * i - 1)
        place = lax.broadcasted_iota(jnp.int32, (span, rows), 0)
        key_at = jnp.concatenate([slot_ref[slot] * span + place for slot in slots], axis=0)
        query_at = mine * rows + lax.broadcasted_iota(jnp.int32, (2 * span, rows), 1)
        fold(slots, (key_at <= query_at) & (key_at >= begin_ref[...]))
        return carry

    def plain_step(i, carry):
        fold((2 * i, 2 * i + 1), None)
        return carry

    lax.fori_loop(0, (masked + 1) // 2, masked_step, 0)
    lax.fori_loop(0, plain // 2, plain_step, 0)
    for h in range(heads):
        at = slice(h * rows, (h + 1) * rows)
        out_ref[:, h * HEAD : (h + 1) * HEAD] = (mix_ref[:, at] / sum_ref[:, at]).T.astype(BF16)


def output_kernel(places, row_ref, col_ref, att_ref, *refs):
    pieces, out_ref = refs[:-1], refs[-1]
    count, _, width = pieces[0].shape
    for k in range(count):
        total = None
        for (core, x), piece in zip(places, pieces):
            part = jnp.dot(
                att_ref[row_ref[core * 4 + x]], piece[k], preferred_element_type=F32
            )
            total = part if total is None else total + part
        col = pl.ds(pl.multiple_of(col_ref[k] * width, width), width)
        out_ref[:, col] = total.astype(BF16)


def row_kernel(in_ref, out_ref):
    out_ref[...] = in_ref[...]


def finish_kernel(hidden_ref, landed_ref, out_ref):
    count, _, cols = landed_ref.shape
    width = cols // 4
    for j in range(4):
        for c in range(count):
            at = slice((j * count + c) * width, (j * count + c + 1) * width)
            part = landed_ref[c, :, j * width : (j + 1) * width]
            out_ref[:, at] = hidden_ref[:, at].astype(F32) + part.astype(F32)


def shards(hidden, norm_gain, w_query, w_key, w_value, bias_query, bias_key, bias_value, w_out, seq_lengths):
    rows, width = hidden.shape
    zh, x, co, y, zl = (lax.axis_index(a) for a in ALL)
    mine = (zh * 4 + x) * 2 + co
    off = jnp.array([o % 4 for o in OFFSETS], jnp.int32)
    src_z, src_x = (zh + off) % 4, (x + off) % 4
    src_c = jnp.stack([co, 1 - co])
    all_4 = jnp.arange(4, dtype=jnp.int32)

    def table(x_at, z_at):
        places = z_at[None, None, :] * 8 + x_at[None, :, None] * 2 + src_c[:, None, None]
        return places.reshape(32).astype(jnp.int32)

    q_order, kv_order, block_order = table(src_x, src_z), table(all_4, all_4), table(src_x, all_4)

    moves = []
    for d in range(256):
        l = d % 2
        yy = d // 2 % 4
        c = d // 8 % 2
        xx = d // 16 % 4
        zz = d // 64
        moves.append((d, (((zz * 4 + (xx + yy) % 4) * 2 + l) * 4 + xx) * 2 + c))
    pick_key = zl == 0
    at = y * HEAD
    kv_block = jnp.where(
        pick_key,
        lax.dynamic_slice_in_dim(w_key, at, HEAD, 1),
        lax.dynamic_slice_in_dim(w_value, at, HEAD, 1),
    )
    kv_bias = jnp.where(
        pick_key,
        lax.dynamic_slice_in_dim(bias_key, at, HEAD, 0),
        lax.dynamic_slice_in_dim(bias_value, at, HEAD, 0),
    )
    kv_stack = spread(spread(kv_block, "zh", 4), "x", 4).reshape(16, -1, HEAD)
    kv_weights = both_cores([kv_stack])
    q_stack = jnp.stack(ring_gather(w_query, "zh"))
    q_weights = both_cores(ring_gather(q_stack, "x"))
    out_block = lax.ppermute(w_out, ALL, moves)
    out_stack = jnp.stack(ring_gather(out_block, "zh"))
    out_weights = both_cores(ring_gather(out_stack, "x"))

    ends = jnp.cumsum(seq_lengths)
    index = mine * rows + jnp.arange(rows, dtype=jnp.int32)
    begin = jnp.max(jnp.where(index[:, None] >= ends[None, :], ends[None, :], 0), axis=1).astype(jnp.int32)
    position = (index - begin).astype(F32)
    frequency = jnp.exp(jnp.arange(HEAD // 2, dtype=F32) * (-2.0 * math.log(ROPE_BASE) / HEAD))
    angle = position[:, None] * frequency[None, :]
    cos, sin = jnp.cos(angle), jnp.sin(angle)
    cos = jnp.concatenate([cos, cos], axis=1)
    sin = jnp.concatenate([-sin, sin], axis=1)
    kv_cos = jnp.where(pick_key, cos, 1.0)
    kv_sin = jnp.where(pick_key, sin, 0.0)

    def project(pieces, order, bias, cos, sin):
        cols = bias.shape[0]
        return call(
            functools.partial(project_kernel, [p[:3] for p in pieces]),
            jax.ShapeDtypeStruct((rows, cols), BF16),
            (
                order,
                hidden,
                norm_gain[None, :],
                bias.astype(F32)[None, :],
                cos,
                sin,
                *[p[3] for p in pieces],
            ),
            scratch=[pltpu.VMEM((rows, width), BF16)],
            smem_count=1,
            extra=rows * width * 2,
            flops=2 * rows * width * cols,
            moved=2 * width * (rows + cols),
        )

    kv_own = project(kv_weights, kv_order, kv_bias, kv_cos, kv_sin)
    kv_other = swap(kv_own, "zl")
    kv_pair = jnp.concatenate(
        [jnp.where(pick_key, kv_own, kv_other), jnp.where(pick_key, kv_other, kv_own)], axis=1
    )
    kv_stack = spread(kv_pair, "zh", 4)
    kv = both_cores(ring_gather(kv_stack, "x"))
    query = project(q_weights, q_order, bias_query, cos, sin)
    begin_row = call(row_kernel, jax.ShapeDtypeStruct((1, rows), jnp.int32), (begin[None, :],))
    info = jnp.stack([mine, begin[0] // rows, (begin[rows - 1] + rows - 1) // rows]).astype(jnp.int32)
    heads = query.shape[1] // HEAD
    attended = call(
        functools.partial(attend_kernel, [p[:3] for p in kv]),
        jax.ShapeDtypeStruct(query.shape, BF16),
        (block_order, info, query, begin_row, *[p[3] for p in kv]),
        scratch=[
            pltpu.VMEM((34, rows, HEAD), BF16),
            pltpu.VMEM((34, HEAD, rows), BF16),
            pltpu.SMEM((34,), jnp.int32),
            pltpu.VMEM((2, 2 * rows, rows), F32),
            pltpu.VMEM((1, heads * rows), F32),
            pltpu.VMEM((1, heads * rows), F32),
            pltpu.VMEM((HEAD, heads * rows), F32),
        ],
        smem_count=2,
        extra=10 << 20,
        flops=4 * heads * rows * 6144 * HEAD * 2,
        moved=5 * 1024 * 1024,
        transcendentals=heads * rows * 6144,
    )

    parts = spread(attended, TP, 8)
    row_of = (((src_x - y) % 4)[None, :] * 2 + src_c[:, None]).reshape(8).astype(jnp.int32)
    cols = width // 8
    mixed = call(
        functools.partial(output_kernel, [p[:2] for p in out_weights]),
        jax.ShapeDtypeStruct((rows, cols), BF16),
        (row_of, src_z.astype(jnp.int32), parts, *[p[3] for p in out_weights]),
        smem_count=2,
        flops=2 * rows * cols * 4096,
        moved=12 * 1024 * 1024,
    )
    share = rows // 8
    landed = lax.all_to_all(mixed.reshape(8, share, cols), TP, 0, 0, tiled=True)
    own = lax.dynamic_slice_in_dim(hidden, (y * 2 + zl) * share, share, 0)
    return call(
        finish_kernel,
        jax.ShapeDtypeStruct((share, width), F32),
        (own, landed),
        flops=2 * share * width,
        moved=8 * share * width,
    )


def solution(mesh):
    fine = Mesh(mesh.devices.reshape(4, 4, 2, 4, 2), ALL)

    return jax.shard_map(
        shards,
        mesh=fine,
        in_specs=(
            P(FSDP, None),
            P(),
            P(FSDP, TP),
            P(FSDP, None),
            P(FSDP, None),
            P(TP),
            P(),
            P(),
            P(TP, FSDP),
            P(),
        ),
        out_specs=P(ALL, None),
        check_vma=False,
    )
```

profile of v0, /device:TPU:1, one launch (start us, length us, event | category | flops | bytes accessed | tf_op | source)
XLA Modules:
  0.0 286.3 jit_solution(2624860333863082652)
XLA Ops:
  1.7 9.1 %all-to-all-start = ((bf16[4,256,128]{2,1,0:T(8,128)(2,1)}), bf16[4,256,128]{2,1,0:T(8,128)(2,1)S(1)}, u32[]{:S(2)}, u32[]{:S(2)}) async-start(bf16[4,256,128]{2,1,0:T(8,128)(2,1)} %broadcast_in_dim.46), calls=%async_computation | async-start | bytes 524288 | tf_op jit(solution)/shard_map/all_to_all | solution.py:65
  10.8 3.6 %collective-permute-start.1 = (bf16[256,512]{1,0:T(8,128)(2,1)}, bf16[256,512]{1,0:T(8,128)(2,1)S(1)}, u32[]{:S(2)}, u32[]{:S(2)}) collective-permute-start(bf16[256,512]{1,0:T(8,128)(2,1)} %param.13), channel_id=1, source_target_pairs={{0,192},{64,0},{128,64},{192,128},{1,193},{65,1},{129,65},{193,129... | collective-permute-start | bytes 786440 | tf_op jit(solution)/shard_map/ppermute | solution.py:52
  14.5 4.6 %all-to-all-done = bf16[4,256,128]{2,1,0:T(8,128)(2,1)S(1)} async-done(((bf16[4,256,128]{2,1,0:T(8,128)(2,1)}), bf16[4,256,128]{2,1,0:T(8,128)(2,1)S(1)}, u32[]{:S(2)}, u32[]{:S(2)}) %all-to-all-start) | async-done | bytes 262176 | tf_op jit(solution)/shard_map/all_to_all | solution.py:65
  20.3 4.0 %all-to-all-start.1 = ((bf16[4,4,256,128]{3,2,1,0:T(8,128)(2,1)}), bf16[4,4,256,128]{3,2,1,0:T(8,128)(2,1)S(1)}, u32[]{:S(2)}, u32[]{:S(2)}) async-start(bf16[4,4,256,128]{3,2,1,0:T(8,128)(2,1)} %broadcast_in_dim.84), calls=%async_computation.1 | async-start | bytes 2097152 | tf_op jit(solution)/shard_map/all_to_all | solution.py:65
  24.6 9.4 %all-to-all-done.1 = bf16[4,4,256,128]{3,2,1,0:T(8,128)(2,1)S(1)} async-done(((bf16[4,4,256,128]{3,2,1,0:T(8,128)(2,1)}), bf16[4,4,256,128]{3,2,1,0:T(8,128)(2,1)S(1)}, u32[]{:S(2)}, u32[]{:S(2)}) %all-to-all-start.1) | async-done | bytes 1048608 | tf_op jit(solution)/shard_map/all_to_all | solution.py:65
  34.0 6.7 %collective-permute-start.12 = (bf16[16,256,128]{2,1,0:T(8,128)(2,1)S(1)}, bf16[16,256,128]{2,1,0:T(8,128)(2,1)}, u32[]{:S(2)}, u32[]{:S(2)}) collective-permute-start(bf16[16,256,128]{2,1,0:T(8,128)(2,1)S(1)} %bitcast.29), channel_id=1, source_target_pairs={{0,8},{8,0},{1,9},{9,1},{2,10},{10,2},{3,11},{11,3},{4,12},{12,4},... | collective-permute-start | bytes 3145736 | tf_op jit(solution)/shard_map/ppermute | solution.py:56
  42.1 2.7 collective-permute-start.3
  45.1 5.8 %collective-permute-done.3 = bf16[128,512]{1,0:T(8,128)(2,1)S(1)} collective-permute-done((bf16[128,512]{1,0:T(8,128)(2,1)S(1)}, bf16[128,512]{1,0:T(8,128)(2,1)S(1)}, u32[]{:S(2)}, u32[]{:S(2)}) %collective-permute-start.3) | collective-permute-done | bytes 131104 | tf_op jit(solution)/shard_map/ppermute | solution.py:52
  50.9 3.6 %collective-permute-done.2 = bf16[128,512]{1,0:T(8,128)(2,1)S(1)} collective-permute-done((bf16[128,512]{1,0:T(8,128)(2,1)S(1)}, bf16[128,512]{1,0:T(8,128)(2,1)S(1)}, u32[]{:S(2)}, u32[]{:S(2)}) %collective-permute-start.2) | collective-permute-done | bytes 131104 | tf_op jit(solution)/shard_map/ppermute | solution.py:52
  60.9 4.5 %shard_map.111 = bf16[256,128]{1,0:T(8,128)(2,1)S(1)} custom-call(s32[32]{0:T(128)S(1)} %add.213.order_ref, bf16[256,8192]{1,0:T(8,128)(2,1)S(1)} %copy-done, f32[1,8192]{1,0:T(1,128)S(1)} %bitcast.32, f32[1,128]{1,0:T(1,128)S(1)} %fusion.6.bias_ref, f32[256,128]{1,0:T(8,128)S(1)} %get-tuple-element.31.cos_ref, f32[256,128]{1,0:T(8,128)S(1)} %get-tuple-element.5.sin_ref, ...), custom_call_target="tpu_custom_call" | custom-call | flops 536870912 | bytes 6291456 | tf_op jit(solution)/shard_map/pallas_call | solution.py:34
  65.4 3.5 %collective-permute-done.13 = bf16[256,128]{1,0:T(8,128)(2,1)S(1)} collective-permute-done((bf16[256,128]{1,0:T(8,128)(2,1)S(1)}, bf16[256,128]{1,0:T(8,128)(2,1)S(1)}, u32[]{:S(2)}, u32[]{:S(2)}) %collective-permute-start.13) | collective-permute-done | bytes 65568 | tf_op jit(solution)/shard_map/ppermute | solution.py:56
  69.8 4.1 %all-to-all-start.2 = ((bf16[4,256,256]{2,1,0:T(8,128)(2,1)}), bf16[4,256,256]{2,1,0:T(8,128)(2,1)}, u32[]{:S(2)}, u32[]{:S(2)}) async-start(bf16[4,256,256]{2,1,0:T(8,128)(2,1)} %broadcast_in_dim.85), calls=%async_computation.2 | async-start | bytes 1048576 | tf_op jit(solution)/shard_map/all_to_all | solution.py:65
  74.0 5.6 %collective-permute-done.4.refs_1_ = bf16[4,256,512]{2,1,0:T(8,128)(2,1)S(1)} collective-permute-done((bf16[4,256,512]{2,1,0:T(8,128)(2,1)S(1)}, bf16[4,256,512]{2,1,0:T(8,128)(2,1)S(1)}, u32[]{:S(2)}, u32[]{:S(2)}) %collective-permute-start.4) | collective-permute-done | bytes 1048608 | tf_op jit(solution)/shard_map/ppermute | solution.py:52
  84.9 2.7 collective-permute-start.15
  87.6 6.6 %collective-permute-start.8 = (bf16[4,256,512]{2,1,0:T(8,128)(2,1)S(1)}, bf16[4,256,512]{2,1,0:T(8,128)(2,1)S(1)}, u32[]{:S(2)}, u32[]{:S(2)}) collective-permute-start(bf16[4,256,512]{2,1,0:T(8,128)(2,1)S(1)} %pad_maximum_fusion.refs_0_), channel_id=1, source_target_pairs={{0,8},{8,0},{1,9},{9,1},{2,10},{10,2},{3,11},{11,3},{4,12},{12,4},... | collective-permute-start | bytes 3145736 | tf_op jit(solution)/shard_map/ppermute | solution.py:56
  94.2 4.4 %collective-permute-start.9 = (bf16[4,256,512]{2,1,0:T(8,128)(2,1)S(1)}, bf16[4,256,512]{2,1,0:T(8,128)(2,1)S(1)}, u32[]{:S(2)}, u32[]{:S(2)}) collective-permute-start(bf16[4,256,512]{2,1,0:T(8,128)(2,1)S(1)} %collective-permute-done.4.refs_1_), channel_id=1, source_target_pairs={{0,8},{8,0},{1,9},{9,1},{2,10},{10,2},{3,11},{11,3},{4,12},{12,4},... | collective-permute-start | bytes 3145736 | tf_op jit(solution)/shard_map/ppermute | solution.py:56
  104.6 2.9 collective-permute-start.11
  109.5 7.6 %collective-permute-done.16 = bf16[2,256,256]{2,1,0:T(8,128)(2,1)S(1)} collective-permute-done((bf16[2,256,256]{2,1,0:T(8,128)(2,1)S(1)}, bf16[2,256,256]{2,1,0:T(8,128)(2,1)S(1)}, u32[]{:S(2)}, u32[]{:S(2)}) %collective-permute-start.16) | collective-permute-done | bytes 262176 | tf_op jit(solution)/shard_map/ppermute | solution.py:52
  117.8 5.7 %collective-permute-done.17 = bf16[2,256,256]{2,1,0:T(8,128)(2,1)S(1)} collective-permute-done((bf16[2,256,256]{2,1,0:T(8,128)(2,1)S(1)}, bf16[2,256,256]{2,1,0:T(8,128)(2,1)S(1)}, u32[]{:S(2)}, u32[]{:S(2)}) %collective-permute-start.17) | collective-permute-done | bytes 262176 | tf_op jit(solution)/shard_map/ppermute | solution.py:52
  142.0 5.9 %shard_map.109.query_ref = bf16[256,512]{1,0:T(8,128)(2,1)S(1)} custom-call(s32[32]{0:T(128)S(1)} %add.208.order_ref, bf16[256,8192]{1,0:T(8,128)(2,1)S(1)} %copy-done.1, f32[1,8192]{1,0:T(1,128)S(1)} %bitcast.33, f32[1,512]{1,0:T(1,128)S(1)} %bitcast.35, f32[256,128]{1,0:T(8,128)S(1)} %get-tuple-element.30.cos_ref, ...), custom_call_target="tpu_custom_call" | custom-call | flops 2147483648 | bytes 12582912 | tf_op jit(solution)/shard_map/pallas_call | solution.py:34
  148.0 4.1 %shard_map.112 = bf16[256,512]{1,0:T(8,128)(2,1)S(1)} custom-call(s32[32]{0:T(128)S(1)} %add.199.block_ref, s32[3]{0:T(128)S(1)} %pad_add_fusion.1.info_ref, bf16[256,512]{1,0:T(8,128)(2,1)S(1)} %shard_map.109.query_ref, s32[1,256]{1,0:T(1,128)S(1)} %shard_map.110.begin_ref, bf16[4,256,256]{2,1,0:T(8,128)(2,1)} %all-to-all-done.2.refs_0_, ...), custom_call_target="tpu_custom_call" | custom-call | flops 6442450944 | bytes 5242880 | tf_op jit(solution)/shard_map/pallas_call | solution.py:34
  153.6 4.4 %all-to-all-start.3 = ((bf16[8,256,512]{2,1,0:T(8,128)(2,1)}), bf16[8,256,512]{2,1,0:T(8,128)(2,1)S(1)}, u32[]{:S(2)}, u32[]{:S(2)}) async-start(bf16[8,256,512]{2,1,0:T(8,128)(2,1)} %broadcast_in_dim.86), calls=%async_computation.3 | async-start | bytes 4194304 | tf_op jit(solution)/shard_map/all_to_all | solution.py:65
  158.0 12.8 %collective-permute-start.24 = (bf16[512,256]{1,0:T(8,128)(2,1)}, bf16[512,256]{1,0:T(8,128)(2,1)S(1)}, u32[]{:S(2)}, u32[]{:S(2)}) collective-permute-start(bf16[512,256]{1,0:T(8,128)(2,1)} %collective-permute-done.22), channel_id=1, source_target_pairs={{0,192},{64,0},{128,64},{192,128},{1,193},{65,1},{129,65},{193,129... | collective-permute-start | bytes 786440 | tf_op jit(solution)/shard_map/ppermute | solution.py:52
  170.8 6.5 %collective-permute-done.24 = bf16[512,256]{1,0:T(8,128)(2,1)S(1)} collective-permute-done((bf16[512,256]{1,0:T(8,128)(2,1)}, bf16[512,256]{1,0:T(8,128)(2,1)S(1)}, u32[]{:S(2)}, u32[]{:S(2)}) %collective-permute-start.24) | collective-permute-done | bytes 262176 | tf_op jit(solution)/shard_map/ppermute | solution.py:52
  177.3 4.3 %collective-permute-start.26 = (bf16[256,256]{1,0:T(8,128)(2,1)S(1)}, bf16[256,256]{1,0:T(8,128)(2,1)S(1)}, u32[]{:S(2)}, u32[]{:S(2)}) collective-permute-start(bf16[256,256]{1,0:T(8,128)(2,1)S(1)} %slice.55), channel_id=1, source_target_pairs={{0,192},{64,0},{128,64},{192,128},{1,193},{65,1},{129,65},{193,129... | collective-permute-start | bytes 393224 | tf_op jit(solution)/shard_map/ppermute | solution.py:52
  181.5 24.2 %collective-permute-done.23 = bf16[512,256]{1,0:T(8,128)(2,1)S(1)} collective-permute-done((bf16[512,256]{1,0:T(8,128)(2,1)}, bf16[512,256]{1,0:T(8,128)(2,1)S(1)}, u32[]{:S(2)}, u32[]{:S(2)}) %collective-permute-start.23) | collective-permute-done | bytes 262176 | tf_op jit(solution)/shard_map/ppermute | solution.py:52
  205.9 6.8 %collective-permute-done.25 = bf16[256,256]{1,0:T(8,128)(2,1)S(1)} collective-permute-done((bf16[256,256]{1,0:T(8,128)(2,1)S(1)}, bf16[256,256]{1,0:T(8,128)(2,1)S(1)}, u32[]{:S(2)}, u32[]{:S(2)}) %collective-permute-start.25) | collective-permute-done | bytes 131104 | tf_op jit(solution)/shard_map/ppermute | solution.py:52
  216.5 22.1 %collective-permute-done.27.refs_1_ = bf16[4,512,256]{2,1,0:T(8,128)(2,1)} collective-permute-done((bf16[4,512,256]{2,1,0:T(8,128)(2,1)S(1)}, bf16[4,512,256]{2,1,0:T(8,128)(2,1)}, u32[]{:S(2)}, u32[]{:S(2)}) %collective-permute-start.27) | collective-permute-done | bytes 1048608 | tf_op jit(solution)/shard_map/ppermute | solution.py:52
  246.8 7.5 %collective-permute-done.29 = bf16[2,512,256]{2,1,0:T(8,128)(2,1)S(1)} collective-permute-done((bf16[2,512,256]{2,1,0:T(8,128)(2,1)S(1)}, bf16[2,512,256]{2,1,0:T(8,128)(2,1)S(1)}, u32[]{:S(2)}, u32[]{:S(2)}) %collective-permute-start.29) | collective-permute-done | bytes 524320 | tf_op jit(solution)/shard_map/ppermute | solution.py:52
  261.5 5.5 %shard_map.113 = bf16[256,1024]{1,0:T(8,128)(2,1)S(1)} custom-call(s32[8]{0:T(128)S(1)} %add.189.row_ref, s32[4]{0:T(128)S(1)} %get-tuple-element.8.col_ref, bf16[8,256,512]{2,1,0:T(8,128)(2,1)S(1)} %all-to-all-done.3.att_ref, bf16[4,512,256]{2,1,0:T(8,128)(2,1)S(1)} %pad_maximum_fusion.1.refs_0_, bf16[4,512,256]{2,1,0:T(8,128)(2,1)} %collective-permute-done.27.refs_1_, ...), custom_call_target="tpu_custom_call" | custom-call | flops 2147483648 | bytes 12582912 | tf_op jit(solution)/shard_map/pallas_call | solution.py:34
  267.8 8.2 %all-to-all-start.4 = ((bf16[8,32,1024]{2,1,0:T(8,128)(2,1)}), bf16[8,32,1024]{2,1,0:T(8,128)(2,1)S(1)}, u32[]{:S(2)}, u32[]{:S(2)}) async-start(bf16[8,32,1024]{2,1,0:T(8,128)(2,1)} %bitcast.31), calls=%async_computation.4 | async-start | bytes 1048576 | tf_op jit(solution)/shard_map/all_to_all | solution.py:377
  277.1 8.2 %all-to-all-done.4.landed_ref = bf16[8,32,1024]{2,1,0:T(8,128)(2,1)S(1)} async-done(((bf16[8,32,1024]{2,1,0:T(8,128)(2,1)}), bf16[8,32,1024]{2,1,0:T(8,128)(2,1)S(1)}, u32[]{:S(2)}, u32[]{:S(2)}) %all-to-all-start.4) | async-done | bytes 524320 | tf_op jit(solution)/shard_map/all_to_all | solution.py:377
  (140 shorter events, 65.3 us)
Async XLA Ops:
  1.7 17.4 %all-to-all-start = ((bf16[4,256,128]{2,1,0:T(8,128)(2,1)}), bf16[4,256,128]{2,1,0:T(8,128)(2,1)S(1)}, u32[]{:S(2)}, u32[]{:S(2)}) async-start(bf16[4,256,128]{2,1,0:T(8,128)(2,1)} %broadcast_in_dim.46), calls=%async_computation | async-start | bytes 524288 | tf_op jit(solution)/shard_map/all_to_all | solution.py:65
  10.8 31.2 %collective-permute-start.1 = (bf16[256,512]{1,0:T(8,128)(2,1)}, bf16[256,512]{1,0:T(8,128)(2,1)S(1)}, u32[]{:S(2)}, u32[]{:S(2)}) collective-permute-start(bf16[256,512]{1,0:T(8,128)(2,1)} %param.13), channel_id=1, source_target_pairs={{0,192},{64,0},{128,64},{192,128},{1,193},{65,1},{129,65},{193,129... | collective-permute-start | bytes 786440 | tf_op jit(solution)/shard_map/ppermute | solution.py:52
  14.4 30.4 %collective-permute-start = (bf16[256,512]{1,0:T(8,128)(2,1)}, bf16[256,512]{1,0:T(8,128)(2,1)S(1)}, u32[]{:S(2)}, u32[]{:S(2)}) collective-permute-start(bf16[256,512]{1,0:T(8,128)(2,1)} %param.13), channel_id=1, source_target_pairs={{0,64},{64,128},{128,192},{192,0},{1,65},{65,129},{129,193},{193,1... | collective-permute-start | bytes 786440 | tf_op jit(solution)/shard_map/ppermute | solution.py:52
  20.3 13.8 %all-to-all-start.1 = ((bf16[4,4,256,128]{3,2,1,0:T(8,128)(2,1)}), bf16[4,4,256,128]{3,2,1,0:T(8,128)(2,1)S(1)}, u32[]{:S(2)}, u32[]{:S(2)}) async-start(bf16[4,4,256,128]{3,2,1,0:T(8,128)(2,1)} %broadcast_in_dim.84), calls=%async_computation.1 | async-start | bytes 2097152 | tf_op jit(solution)/shard_map/all_to_all | solution.py:65
  34.0 24.6 %collective-permute-start.12 = (bf16[16,256,128]{2,1,0:T(8,128)(2,1)S(1)}, bf16[16,256,128]{2,1,0:T(8,128)(2,1)}, u32[]{:S(2)}, u32[]{:S(2)}) collective-permute-start(bf16[16,256,128]{2,1,0:T(8,128)(2,1)S(1)} %bitcast.29), channel_id=1, source_target_pairs={{0,8},{8,0},{1,9},{9,1},{2,10},{10,2},{3,11},{11,3},{4,12},{12,4},... | collective-permute-start | bytes 3145736 | tf_op jit(solution)/shard_map/ppermute | solution.py:56
  54.7 24.9 %collective-permute-start.4 = (bf16[4,256,512]{2,1,0:T(8,128)(2,1)S(1)}, bf16[4,256,512]{2,1,0:T(8,128)(2,1)S(1)}, u32[]{:S(2)}, u32[]{:S(2)}) collective-permute-start(bf16[4,256,512]{2,1,0:T(8,128)(2,1)S(1)} %pad_maximum_fusion.refs_0_), channel_id=1, source_target_pairs={{0,16},{16,32},{32,48},{48,0},{1,17},{17,33},{33,49},{49,1},{2,18}... | collective-permute-start | bytes 3145736 | tf_op jit(solution)/shard_map/ppermute | solution.py:52
  55.0 25.3 %collective-permute-start.5 = (bf16[4,256,512]{2,1,0:T(8,128)(2,1)S(1)}, bf16[4,256,512]{2,1,0:T(8,128)(2,1)}, u32[]{:S(2)}, u32[]{:S(2)}) collective-permute-start(bf16[4,256,512]{2,1,0:T(8,128)(2,1)S(1)} %pad_maximum_fusion.refs_0_), channel_id=1, source_target_pairs={{0,48},{16,0},{32,16},{48,32},{1,49},{17,1},{33,17},{49,33},{2,50}... | collective-permute-start | bytes 3145736 | tf_op jit(solution)/shard_map/ppermute | solution.py:52
  69.8 15.1 %all-to-all-start.2 = ((bf16[4,256,256]{2,1,0:T(8,128)(2,1)}), bf16[4,256,256]{2,1,0:T(8,128)(2,1)}, u32[]{:S(2)}, u32[]{:S(2)}) async-start(bf16[4,256,256]{2,1,0:T(8,128)(2,1)} %broadcast_in_dim.85), calls=%async_computation.2 | async-start | bytes 1048576 | tf_op jit(solution)/shard_map/all_to_all | solution.py:65
  80.4 13.8 %collective-permute-start.6 = (bf16[2,256,512]{2,1,0:T(8,128)(2,1)}, bf16[2,256,512]{2,1,0:T(8,128)(2,1)S(1)}, u32[]{:S(2)}, u32[]{:S(2)}) collective-permute-start(bf16[2,256,512]{2,1,0:T(8,128)(2,1)} %slice.50), channel_id=1, source_target_pairs={{0,16},{16,32},{32,48},{48,0},{1,17},{17,33},{33,49},{49,1},{2,18}... | collective-permute-start | bytes 1572872 | tf_op jit(solution)/shard_map/ppermute | solution.py:52
  82.2 16.3 %collective-permute-start.7 = (bf16[2,256,512]{2,1,0:T(8,128)(2,1)}, bf16[2,256,512]{2,1,0:T(8,128)(2,1)S(1)}, u32[]{:S(2)}, u32[]{:S(2)}) collective-permute-start(bf16[2,256,512]{2,1,0:T(8,128)(2,1)} %slice.51), channel_id=1, source_target_pairs={{0,48},{16,0},{32,16},{48,32},{1,49},{17,1},{33,17},{49,33},{2,50}... | collective-permute-start | bytes 1572872 | tf_op jit(solution)/shard_map/ppermute | solution.py:52
  84.9 19.7 %collective-permute-start.14 = (bf16[4,256,256]{2,1,0:T(8,128)(2,1)}, bf16[4,256,256]{2,1,0:T(8,128)(2,1)}, u32[]{:S(2)}, u32[]{:S(2)}) collective-permute-start(bf16[4,256,256]{2,1,0:T(8,128)(2,1)} %all-to-all-done.2.refs_0_), channel_id=1, source_target_pairs={{0,16},{16,32},{32,48},{48,0},{1,17},{17,33},{33,49},{49,1},{2,18}... | collective-permute-start | bytes 1572872 | tf_op jit(solution)/shard_map/ppermute | solution.py:52
  84.9 23.5 %collective-permute-start.15 = (bf16[4,256,256]{2,1,0:T(8,128)(2,1)}, bf16[4,256,256]{2,1,0:T(8,128)(2,1)}, u32[]{:S(2)}, u32[]{:S(2)}) collective-permute-start(bf16[4,256,256]{2,1,0:T(8,128)(2,1)} %all-to-all-done.2.refs_0_), channel_id=1, source_target_pairs={{0,48},{16,0},{32,16},{48,32},{1,49},{17,1},{33,17},{49,33},{2,50}... | collective-permute-start | bytes 1572872 | tf_op jit(solution)/shard_map/ppermute | solution.py:52
  87.6 38.9 %collective-permute-start.8 = (bf16[4,256,512]{2,1,0:T(8,128)(2,1)S(1)}, bf16[4,256,512]{2,1,0:T(8,128)(2,1)S(1)}, u32[]{:S(2)}, u32[]{:S(2)}) collective-permute-start(bf16[4,256,512]{2,1,0:T(8,128)(2,1)S(1)} %pad_maximum_fusion.refs_0_), channel_id=1, source_target_pairs={{0,8},{8,0},{1,9},{9,1},{2,10},{10,2},{3,11},{11,3},{4,12},{12,4},... | collective-permute-start | bytes 3145736 | tf_op jit(solution)/shard_map/ppermute | solution.py:56
  94.2 33.3 %collective-permute-start.9 = (bf16[4,256,512]{2,1,0:T(8,128)(2,1)S(1)}, bf16[4,256,512]{2,1,0:T(8,128)(2,1)S(1)}, u32[]{:S(2)}, u32[]{:S(2)}) collective-permute-start(bf16[4,256,512]{2,1,0:T(8,128)(2,1)S(1)} %collective-permute-done.4.refs_1_), channel_id=1, source_target_pairs={{0,8},{8,0},{1,9},{9,1},{2,10},{10,2},{3,11},{11,3},{4,12},{12,4},... | collective-permute-start | bytes 3145736 | tf_op jit(solution)/shard_map/ppermute | solution.py:56
  99.4 29.6 %collective-permute-start.10 = (bf16[4,256,512]{2,1,0:T(8,128)(2,1)}, bf16[4,256,512]{2,1,0:T(8,128)(2,1)S(1)}, u32[]{:S(2)}, u32[]{:S(2)}) collective-permute-start(bf16[4,256,512]{2,1,0:T(8,128)(2,1)} %collective-permute-done.5.refs_2_), channel_id=1, source_target_pairs={{0,8},{8,0},{1,9},{9,1},{2,10},{10,2},{3,11},{11,3},{4,12},{12,4},... | collective-permute-start | bytes 3145736 | tf_op jit(solution)/shard_map/ppermute | solution.py:56
  104.6 29.6 %collective-permute-start.11 = (bf16[4,256,512]{2,1,0:T(8,128)(2,1)S(1)}, bf16[4,256,512]{2,1,0:T(8,128)(2,1)}, u32[]{:S(2)}, u32[]{:S(2)}) collective-permute-start(bf16[4,256,512]{2,1,0:T(8,128)(2,1)S(1)} %constant_dynamic-update-slice_fusion.refs_3_), channel_id=1, source_target_pairs={{0,8},{8,0},{1,9},{9,1},{2,10},{10,2},{3,11},{11,3},{4,12},{12,4},... | collective-permute-start | bytes 3145736 | tf_op jit(solution)/shard_map/ppermute | solution.py:56
  123.5 24.4 %collective-permute-start.18 = (bf16[4,256,256]{2,1,0:T(8,128)(2,1)}, bf16[4,256,256]{2,1,0:T(8,128)(2,1)}, u32[]{:S(2)}, u32[]{:S(2)}) collective-permute-start(bf16[4,256,256]{2,1,0:T(8,128)(2,1)} %all-to-all-done.2.refs_0_), channel_id=1, source_target_pairs={{0,8},{8,0},{1,9},{9,1},{2,10},{10,2},{3,11},{11,3},{4,12},{12,4},... | collective-permute-start | bytes 1572872 | tf_op jit(solution)/shard_map/ppermute | solution.py:56
  127.5 20.5 %collective-permute-start.19 = (bf16[4,256,256]{2,1,0:T(8,128)(2,1)}, bf16[4,256,256]{2,1,0:T(8,128)(2,1)}, u32[]{:S(2)}, u32[]{:S(2)}) collective-permute-start(bf16[4,256,256]{2,1,0:T(8,128)(2,1)} %collective-permute-done.14.refs_1_), channel_id=1, source_target_pairs={{0,8},{8,0},{1,9},{9,1},{2,10},{10,2},{3,11},{11,3},{4,12},{12,4},... | collective-permute-start | bytes 1572872 | tf_op jit(solution)/shard_map/ppermute | solution.py:56
  128.5 19.5 %collective-permute-start.20 = (bf16[4,256,256]{2,1,0:T(8,128)(2,1)}, bf16[4,256,256]{2,1,0:T(8,128)(2,1)}, u32[]{:S(2)}, u32[]{:S(2)}) collective-permute-start(bf16[4,256,256]{2,1,0:T(8,128)(2,1)} %collective-permute-done.15.refs_2_), channel_id=1, source_target_pairs={{0,8},{8,0},{1,9},{9,1},{2,10},{10,2},{3,11},{11,3},{4,12},{12,4},... | collective-permute-start | bytes 1572872 | tf_op jit(solution)/shard_map/ppermute | solution.py:56
  130.0 18.0 %collective-permute-start.21 = (bf16[4,256,256]{2,1,0:T(8,128)(2,1)}, bf16[4,256,256]{2,1,0:T(8,128)(2,1)}, u32[]{:S(2)}, u32[]{:S(2)}) collective-permute-start(bf16[4,256,256]{2,1,0:T(8,128)(2,1)} %constant_dynamic-update-slice_fusion.2.refs_3_), channel_id=1, source_target_pairs={{0,8},{8,0},{1,9},{9,1},{2,10},{10,2},{3,11},{11,3},{4,12},{12,4},... | collective-permute-start | bytes 1572872 | tf_op jit(solution)/shard_map/ppermute | solution.py:56
  134.2 23.8 %collective-permute-start.22 = (bf16[512,256]{1,0:T(8,128)(2,1)}, bf16[512,256]{1,0:T(8,128)(2,1)}, u32[]{:S(2)}, u32[]{:S(2)}) collective-permute-start(bf16[512,256]{1,0:T(8,128)(2,1)} %param.19), channel_id=1, source_target_pairs={{0,0},{1,8},{2,16},{3,24},{4,32},{5,40},{6,48},{7,56},{8,1},{9,9},... | collective-permute-start | bytes 786440 | tf_op jit(solution)/shard_map/ppermute | solution.py:297
  153.6 107.9 %all-to-all-start.3 = ((bf16[8,256,512]{2,1,0:T(8,128)(2,1)}), bf16[8,256,512]{2,1,0:T(8,128)(2,1)S(1)}, u32[]{:S(2)}, u32[]{:S(2)}) async-start(bf16[8,256,512]{2,1,0:T(8,128)(2,1)} %broadcast_in_dim.86), calls=%async_computation.3 | async-start | bytes 4194304 | tf_op jit(solution)/shard_map/all_to_all | solution.py:65
  158.0 19.3 %collective-permute-start.24 = (bf16[512,256]{1,0:T(8,128)(2,1)}, bf16[512,256]{1,0:T(8,128)(2,1)S(1)}, u32[]{:S(2)}, u32[]{:S(2)}) collective-permute-start(bf16[512,256]{1,0:T(8,128)(2,1)} %collective-permute-done.22), channel_id=1, source_target_pairs={{0,192},{64,0},{128,64},{192,128},{1,193},{65,1},{129,65},{193,129... | collective-permute-start | bytes 786440 | tf_op jit(solution)/shard_map/ppermute | solution.py:52
  170.8 35.0 %collective-permute-start.23 = (bf16[512,256]{1,0:T(8,128)(2,1)}, bf16[512,256]{1,0:T(8,128)(2,1)S(1)}, u32[]{:S(2)}, u32[]{:S(2)}) collective-permute-start(bf16[512,256]{1,0:T(8,128)(2,1)} %collective-permute-done.22), channel_id=1, source_target_pairs={{0,64},{64,128},{128,192},{192,0},{1,65},{65,129},{129,193},{193,1... | collective-permute-start | bytes 786440 | tf_op jit(solution)/shard_map/ppermute | solution.py:52
  177.3 28.6 %collective-permute-start.26 = (bf16[256,256]{1,0:T(8,128)(2,1)S(1)}, bf16[256,256]{1,0:T(8,128)(2,1)S(1)}, u32[]{:S(2)}, u32[]{:S(2)}) collective-permute-start(bf16[256,256]{1,0:T(8,128)(2,1)S(1)} %slice.55), channel_id=1, source_target_pairs={{0,192},{64,0},{128,64},{192,128},{1,193},{65,1},{129,65},{193,129... | collective-permute-start | bytes 393224 | tf_op jit(solution)/shard_map/ppermute | solution.py:52
  213.8 24.9 %collective-permute-start.27 = (bf16[4,512,256]{2,1,0:T(8,128)(2,1)S(1)}, bf16[4,512,256]{2,1,0:T(8,128)(2,1)}, u32[]{:S(2)}, u32[]{:S(2)}) collective-permute-start(bf16[4,512,256]{2,1,0:T(8,128)(2,1)S(1)} %pad_maximum_fusion.1.refs_0_), channel_id=1, source_target_pairs={{0,16},{16,32},{32,48},{48,0},{1,17},{17,33},{33,49},{49,1},{2,18}... | collective-permute-start | bytes 3145736 | tf_op jit(solution)/shard_map/ppermute | solution.py:52
  216.2 25.5 %collective-permute-start.28 = (bf16[4,512,256]{2,1,0:T(8,128)(2,1)S(1)}, bf16[4,512,256]{2,1,0:T(8,128)(2,1)}, u32[]{:S(2)}, u32[]{:S(2)}) collective-permute-start(bf16[4,512,256]{2,1,0:T(8,128)(2,1)S(1)} %pad_maximum_fusion.1.refs_0_), channel_id=1, source_target_pairs={{0,48},{16,0},{32,16},{48,32},{1,49},{17,1},{33,17},{49,33},{2,50}... | collective-permute-start | bytes 3145736 | tf_op jit(solution)/shard_map/ppermute | solution.py:52
  239.7 14.5 %collective-permute-start.29 = (bf16[2,512,256]{2,1,0:T(8,128)(2,1)S(1)}, bf16[2,512,256]{2,1,0:T(8,128)(2,1)S(1)}, u32[]{:S(2)}, u32[]{:S(2)}) collective-permute-start(bf16[2,512,256]{2,1,0:T(8,128)(2,1)S(1)} %slice.56), channel_id=1, source_target_pairs={{0,16},{16,32},{32,48},{48,0},{1,17},{17,33},{33,49},{49,1},{2,18}... | collective-permute-start | bytes 1572872 | tf_op jit(solution)/shard_map/ppermute | solution.py:52
  242.8 13.2 %collective-permute-start.30 = (bf16[2,512,256]{2,1,0:T(8,128)(2,1)S(1)}, bf16[2,512,256]{2,1,0:T(8,128)(2,1)S(1)}, u32[]{:S(2)}, u32[]{:S(2)}) collective-permute-start(bf16[2,512,256]{2,1,0:T(8,128)(2,1)S(1)} %slice.57), channel_id=1, source_target_pairs={{0,48},{16,0},{32,16},{48,32},{1,49},{17,1},{33,17},{49,33},{2,50}... | collective-permute-start | bytes 1572872 | tf_op jit(solution)/shard_map/ppermute | solution.py:52
  244.6 14.4 %collective-permute-start.31 = (bf16[4,512,256]{2,1,0:T(8,128)(2,1)S(1)}, bf16[4,512,256]{2,1,0:T(8,128)(2,1)}, u32[]{:S(2)}, u32[]{:S(2)}) collective-permute-start(bf16[4,512,256]{2,1,0:T(8,128)(2,1)S(1)} %pad_maximum_fusion.1.refs_0_), channel_id=1, source_target_pairs={{0,8},{8,0},{1,9},{9,1},{2,10},{10,2},{3,11},{11,3},{4,12},{12,4},... | collective-permute-start | bytes 3145736 | tf_op jit(solution)/shard_map/ppermute | solution.py:56
  246.3 12.7 %collective-permute-start.32 = (bf16[4,512,256]{2,1,0:T(8,128)(2,1)}, bf16[4,512,256]{2,1,0:T(8,128)(2,1)}, u32[]{:S(2)}, u32[]{:S(2)}) collective-permute-start(bf16[4,512,256]{2,1,0:T(8,128)(2,1)} %collective-permute-done.27.refs_1_), channel_id=1, source_target_pairs={{0,8},{8,0},{1,9},{9,1},{2,10},{10,2},{3,11},{11,3},{4,12},{12,4},... | collective-permute-start | bytes 3145736 | tf_op jit(solution)/shard_map/ppermute | solution.py:56
  267.8 17.5 %all-to-all-start.4 = ((bf16[8,32,1024]{2,1,0:T(8,128)(2,1)}), bf16[8,32,1024]{2,1,0:T(8,128)(2,1)S(1)}, u32[]{:S(2)}, u32[]{:S(2)}) async-start(bf16[8,32,1024]{2,1,0:T(8,128)(2,1)} %bitcast.31), calls=%async_computation.4 | async-start | bytes 1048576 | tf_op jit(solution)/shard_map/all_to_all | solution.py:377
  (26 other events, 394.0 us)
where the time goes:
time: 288 us; the launch traced here: 286 us
  waiting for transfers between devices  126 us (44%)
  starting transfers between devices  99.2 us (34%)
  local copies, waits for them, and re-layouts  31 us (11%)
  Pallas kernels  21 us (7%)
  other arithmetic  5.5 us (2%)
  between operations  3.74 us (1%)
    ppermute x20, waiting for transfers between devices, shift(): return lax.ppermute(array, axis, [(i, (i + by) % 4) for i in range(4)])  97.7 us
    ppermute x20, starting transfers between devices, shift(): return lax.ppermute(array, axis, [(i, (i + by) % 4) for i in range(4)])  38.2 us
    ppermute x14, starting transfers between devices, swap(): return lax.ppermute(array, axis, [(0, 1), (1, 0)])  29.2 us
    all_to_all x4, starting transfers between devices, spread(): return lax.all_to_all(copies, axes, 0, 0, tiled=True)  21.7 us
    pallas_call x6, Pallas kernels, call(): pl.pallas_call(body, out_shape=out_shape, in_specs=smem(smem_count) + vme...  21 us
    unnamed x39, local copies, waits for them, and re-layouts  15.2 us
    all_to_all x4, waiting for transfers between devices, spread(): return lax.all_to_all(copies, axes, 0, 0, tiled=True)  14 us
    all_to_all x1, starting transfers between devices, shards(): landed = lax.all_to_all(mixed.reshape(8, share, cols), TP, 0, 0, tiled=True)  8.23 us
  transfers between devices with their start and end apart: 40, of which 17 were waited for; matrix products, arithmetic and copies ran while one was open for 8% of the time, Pallas kernels for 5%

commit v1 on v0

--- a/solution.py
+++ b/solution.py
@@ -20,6 +20,8 @@
 BF16 = jnp.bfloat16
 F32 = jnp.float32
 OFFSETS = (0, -1, 1, 2)
+
+Q_ORDER, ROWS, COLS, INFO = 32, 64, 72, 76
 
 
 def vmem(count):
@@ -108,7 +110,7 @@
         out_ref[:, at] = (u * cos_ref[...] + pltpu.roll(u, HEAD // 2, 1) * sin_ref[...]).astype(BF16)
 
 
-def project_kernel(places, order_ref, hidden_ref, gain_ref, bias_ref, cos_ref, sin_ref, *refs):
+def project_kernel(places, base, order_ref, hidden_ref, gain_ref, bias_ref, cos_ref, sin_ref, *refs):
     pieces, out_ref, normed_ref = refs[:-2], refs[-2], refs[-1]
     normalize(hidden_ref, gain_ref, normed_ref)
     total = None
@@ -116,7 +118,7 @@
     for (core, x, z), piece in zip(places, pieces):
         count, rows, cols = piece.shape
         for k in range(0, count, group):
-            taken = [order_ref[(core * 4 + x) * 4 + z + k + i] for i in range(group)]
+            taken = [order_ref[base + (core * 4 + x) * 4 + z + k + i] for i in range(group)]
             part = jnp.dot(
                 jnp.concatenate(
                     [normed_ref[:, pl.ds(pl.multiple_of(t * rows, rows), rows)] for t in taken], axis=1
@@ -128,13 +130,13 @@
     turn_heads(total, bias_ref, cos_ref, sin_ref, out_ref)
 
 
-def attend_kernel(places, block_ref, info_ref, query_ref, begin_ref, *refs):
+def attend_kernel(places, block_ref, query_ref, begin_ref, *refs):
     pieces = refs[: len(places)]
     out_ref, key_ref, value_ref, slot_ref, score_ref, top_ref, sum_ref, mix_ref = refs[len(places) :]
     rows, cols = query_ref.shape
     heads = cols // HEAD
     span = pieces[0].shape[1]
-    mine, lowest, full_from = info_ref[0], info_ref[1], info_ref[2]
+    mine, lowest, full_from = (block_ref[INFO + k] for k in range(3))
     last = key_ref.shape[0] - 1
     rate = HEAD**-0.5 * math.log2(math.e)
 
@@ -227,22 +229,23 @@
         out_ref[:, h * HEAD : (h + 1) * HEAD] = (mix_ref[:, at] / sum_ref[:, at]).T.astype(BF16)
 
 
-def output_kernel(places, row_ref, col_ref, att_ref, *refs):
+def output_kernel(places, row_ref, att_ref, *refs):
     pieces, out_ref = refs[:-1], refs[-1]
     count, _, width = pieces[0].shape
     for k in range(count):
         total = None
         for (core, x), piece in zip(places, pieces):
             part = jnp.dot(
-                att_ref[row_ref[core * 4 + x]], piece[k], preferred_element_type=F32
+                att_ref[row_ref[ROWS + core * 4 + x]], piece[k], preferred_element_type=F32
             )
             total = part if total is None else total + part
-        col = pl.ds(pl.multiple_of(col_ref[k] * width, width), width)
+        col = pl.ds(pl.multiple_of(row_ref[COLS + k] * width, width), width)
         out_ref[:, col] = total.astype(BF16)
 
 
 def row_kernel(in_ref, out_ref):
-    out_ref[...] = in_ref[...]
+    for k in range(in_ref.shape[0]):
+        out_ref[k] = in_ref[k]
 
 
 def finish_kernel(hidden_ref, landed_ref, out_ref):
@@ -310,10 +313,10 @@
     kv_cos = jnp.where(pick_key, cos, 1.0)
     kv_sin = jnp.where(pick_key, sin, 0.0)
 
-    def project(pieces, order, bias, cos, sin):
+    def project(pieces, order, bias, cos, sin, base=0):
         cols = bias.shape[0]
         return call(
-            functools.partial(project_kernel, [p[:3] for p in pieces]),
+            functools.partial(project_kernel, [p[:3] for p in pieces], base),
             jax.ShapeDtypeStruct((rows, cols), BF16),
             (
                 order,
@@ -338,14 +341,22 @@
     )
     kv_stack = spread(kv_pair, "zh", 4)
     kv = both_cores(ring_gather(kv_stack, "x"))
-    query = project(q_weights, q_order, bias_query, cos, sin)
-    begin_row = call(row_kernel, jax.ShapeDtypeStruct((1, rows), jnp.int32), (begin[None, :],))
-    info = jnp.stack([mine, begin[0] // rows, (begin[rows - 1] + rows - 1) // rows]).astype(jnp.int32)
+    row_of = ((src_x - y) % 4)[None, :] * 2 + src_c[:, None]
+    info = jnp.stack([mine, begin[0] // rows, (begin[rows - 1] + rows - 1) // rows])
+    tables = jnp.concatenate([block_order, q_order, row_of.reshape(8), src_z, info]).astype(jnp.int32)
+    tables = pl.pallas_call(
+        row_kernel,
+        out_shape=jax.ShapeDtypeStruct(tables.shape, jnp.int32),
+        in_specs=smem(1),
+        out_specs=smem(1)[0],
+        name="row",
+    )(tables)
+    query = project(q_weights, tables, bias_query, cos, sin, Q_ORDER)
     heads = query.shape[1] // HEAD
     attended = call(
         functools.partial(attend_kernel, [p[:3] for p in kv]),
         jax.ShapeDtypeStruct(query.shape, BF16),
-        (block_order, info, query, begin_row, *[p[3] for p in kv]),
+        (tables, query, begin[None, :], *[p[3] for p in kv]),
         scratch=[
             pltpu.VMEM((34, rows, HEAD), BF16),
             pltpu.VMEM((34, HEAD, rows), BF16),
@@ -355,7 +366,7 @@
             pltpu.VMEM((1, heads * rows), F32),
             pltpu.VMEM((HEAD, heads * rows), F32),
         ],
-        smem_count=2,
+        smem_count=1,
         extra=10 << 20,
         flops=4 * heads * rows * 6144 * HEAD * 2,
         moved=5 * 1024 * 1024,
@@ -363,13 +374,13 @@
     )
 
     parts = spread(attended, TP, 8)
-    row_of = (((src_x - y) % 4)[None, :] * 2 + src_c[:, None]).reshape(8).astype(jnp.int32)
     cols = width // 8
     mixed = call(
         functools.partial(output_kernel, [p[:2] for p in out_weights]),
         jax.ShapeDtypeStruct((rows, cols), BF16),
-        (row_of, src_z.astype(jnp.int32), parts, *[p[3] for p in out_weights]),
-        smem_count=2,
+        (tables, parts, *[p[3] for p in out_weights]),
+        smem_count=1,
+        extra=38 << 20,
         flops=2 * rows * cols * 4096,
         moved=12 * 1024 * 1024,
     )

time: 288 us -> 293 us (1.017)
  waiting for transfers between devices: 126 us -> 121 us
  starting transfers between devices: 99.2 us -> 104 us
  Pallas kernels: 21 us -> 24 us
    ppermute x20, waiting for transfers between devices: 97.7 us -> 86.1 us  [shift(): return lax.ppermute(array, axis, [(i, (i + by) % 4) for i in range(4)])]
    all_to_all x4, waiting for transfers between devices: 14 us -> 24.6 us  [spread(): return lax.all_to_all(copies, axes, 0, 0, tiled=True)]
    ppermute x20, starting transfers between devices: 38.2 us -> 42.2 us  [shift(): return lax.ppermute(array, axis, [(i, (i + by) % 4) for i in range(4)])]
    ppermute x14, waiting for transfers between devices: 5.98 us -> 2.1 us  [swap(): return lax.ppermute(array, axis, [(0, 1), (1, 0)])]
    unnamed x39 -> x55, local copies, waits for them, and re-layouts: 15.2 us -> 18.6 us
    pallas_call x6 -> x5, Pallas kernels: 21 us -> 22.8 us  [call(): pl.pallas_call(body, out_shape=out_shape, in_specs=smem(smem_count) + vme...]
  transfers between devices with their start and end apart: 40 -> 40, of which waited for: 17 -> 16; matrix products, arithmetic and copies ran while one was open for 8% -> 7% of each run, Pallas kernels for 5% -> 5%
where the time goes in v1:
time: 293 us; the launch traced here: 291 us
  waiting for transfers between devices  121 us (41%)
  starting transfers between devices  104 us (35%)
  local copies, waits for them, and re-layouts  32 us (11%)
  Pallas kernels  24 us (8%)
  other arithmetic  6.06 us (2%)
  between operations  3.76 us (1%)
    ppermute x20, waiting for transfers between devices, shift(): return lax.ppermute(array, axis, [(i, (i + by) % 4) for i in range(4)])  86.1 us
    ppermute x20, starting transfers between devices, shift(): return lax.ppermute(array, axis, [(i, (i + by) % 4) for i in range(4)])  42.2 us
    ppermute x14, starting transfers between devices, swap(): return lax.ppermute(array, axis, [(0, 1), (1, 0)])  28 us
    all_to_all x4, waiting for transfers between devices, spread(): return lax.all_to_all(copies, axes, 0, 0, tiled=True)  24.6 us
    pallas_call x5, Pallas kernels, call(): pl.pallas_call(body, out_shape=out_shape, in_specs=smem(smem_count) + vme...  22.8 us
    all_to_all x4, starting transfers between devices, spread(): return lax.all_to_all(copies, axes, 0, 0, tiled=True)  19.6 us
    unnamed x55, local copies, waits for them, and re-layouts  18.6 us
    all_to_all x1, starting transfers between devices, shards(): landed = lax.all_to_all(mixed.reshape(8, share, cols), TP, 0, 0, tiled=True)  9.54 us
  transfers between devices with their start and end apart: 40, of which 16 were waited for; matrix products, arithmetic and copies ran while one was open for 7% of the time, Pallas kernels for 5%

profile of v1, /device:TPU:1, one launch (start us, length us, event | category | flops | bytes accessed | tf_op | source)
XLA Modules:
  0.0 290.7 jit_solution(6650717097953402898)
XLA Ops:
  0.0 6.9 %collective-permute-start.1 = (bf16[256,512]{1,0:T(8,128)(2,1)}, bf16[256,512]{1,0:T(8,128)(2,1)S(1)}, u32[]{:S(2)}, u32[]{:S(2)}) collective-permute-start(bf16[256,512]{1,0:T(8,128)(2,1)} %param.13), channel_id=1, source_target_pairs={{0,192},{64,0},{128,64},{192,128},{1,193},{65,1},{129,65},{193,129... | collective-permute-start | bytes 786440 | tf_op jit(solution)/shard_map/ppermute | solution.py:54
  8.6 5.0 %all-to-all-start = ((bf16[4,256,128]{2,1,0:T(8,128)(2,1)}), bf16[4,256,128]{2,1,0:T(8,128)(2,1)S(1)}, u32[]{:S(2)}, u32[]{:S(2)}) async-start(bf16[4,256,128]{2,1,0:T(8,128)(2,1)} %broadcast_in_dim.46), calls=%async_computation | async-start | bytes 524288 | tf_op jit(solution)/shard_map/all_to_all | solution.py:67
  14.3 8.6 %all-to-all-done = bf16[4,256,128]{2,1,0:T(8,128)(2,1)S(1)} async-done(((bf16[4,256,128]{2,1,0:T(8,128)(2,1)}), bf16[4,256,128]{2,1,0:T(8,128)(2,1)S(1)}, u32[]{:S(2)}, u32[]{:S(2)}) %all-to-all-start) | async-done | bytes 262176 | tf_op jit(solution)/shard_map/all_to_all | solution.py:67
  24.0 4.0 %all-to-all-start.1 = ((bf16[4,4,256,128]{3,2,1,0:T(8,128)(2,1)}), bf16[4,4,256,128]{3,2,1,0:T(8,128)(2,1)S(1)}, u32[]{:S(2)}, u32[]{:S(2)}) async-start(bf16[4,4,256,128]{3,2,1,0:T(8,128)(2,1)} %broadcast_in_dim.84), calls=%async_computation.1 | async-start | bytes 2097152 | tf_op jit(solution)/shard_map/all_to_all | solution.py:67
  28.4 9.4 %all-to-all-done.1 = bf16[4,4,256,128]{3,2,1,0:T(8,128)(2,1)S(1)} async-done(((bf16[4,4,256,128]{3,2,1,0:T(8,128)(2,1)}), bf16[4,4,256,128]{3,2,1,0:T(8,128)(2,1)S(1)}, u32[]{:S(2)}, u32[]{:S(2)}) %all-to-all-start.1) | async-done | bytes 1048608 | tf_op jit(solution)/shard_map/all_to_all | solution.py:67
  37.8 7.4 %collective-permute-start.12 = (bf16[16,256,128]{2,1,0:T(8,128)(2,1)S(1)}, bf16[16,256,128]{2,1,0:T(8,128)(2,1)}, u32[]{:S(2)}, u32[]{:S(2)}) collective-permute-start(bf16[16,256,128]{2,1,0:T(8,128)(2,1)S(1)} %bitcast.29), channel_id=1, source_target_pairs={{0,8},{8,0},{1,9},{9,1},{2,10},{10,2},{3,11},{11,3},{4,12},{12,4},... | collective-permute-start | bytes 3145736 | tf_op jit(solution)/shard_map/ppermute | solution.py:58
  46.5 5.3 %collective-permute-start.3 = (bf16[128,512]{1,0:T(8,128)(2,1)S(1)}, bf16[128,512]{1,0:T(8,128)(2,1)S(1)}, u32[]{:S(2)}, u32[]{:S(2)}) collective-permute-start(bf16[128,512]{1,0:T(8,128)(2,1)S(1)} %slice.49), channel_id=1, source_target_pairs={{0,192},{64,0},{128,64},{192,128},{1,193},{65,1},{129,65},{193,129... | collective-permute-start | bytes 393224 | tf_op jit(solution)/shard_map/ppermute | solution.py:54
  52.0 6.3 %collective-permute-done.3 = bf16[128,512]{1,0:T(8,128)(2,1)S(1)} collective-permute-done((bf16[128,512]{1,0:T(8,128)(2,1)S(1)}, bf16[128,512]{1,0:T(8,128)(2,1)S(1)}, u32[]{:S(2)}, u32[]{:S(2)}) %collective-permute-start.3) | collective-permute-done | bytes 131104 | tf_op jit(solution)/shard_map/ppermute | solution.py:54
  65.4 4.5 %shard_map.110 = bf16[256,128]{1,0:T(8,128)(2,1)S(1)} custom-call(s32[32]{0:T(128)S(1)} %add.213.order_ref, bf16[256,8192]{1,0:T(8,128)(2,1)S(1)} %copy-done, f32[1,8192]{1,0:T(1,128)S(1)} %bitcast.31, f32[1,128]{1,0:T(1,128)S(1)} %fusion.6.bias_ref, f32[256,128]{1,0:T(8,128)S(1)} %get-tuple-element.31.cos_ref, f32[256,128]{1,0:T(8,128)S(1)} %get-tuple-element.5.sin_ref, ...), custom_call_target="tpu_custom_call" | custom-call | flops 536870912 | bytes 6291456 | tf_op jit(solution)/shard_map/pallas_call | solution.py:36
  75.1 6.0 %all-to-all-start.2 = ((bf16[4,256,256]{2,1,0:T(8,128)(2,1)}), bf16[4,256,256]{2,1,0:T(8,128)(2,1)}, u32[]{:S(2)}, u32[]{:S(2)}) async-start(bf16[4,256,256]{2,1,0:T(8,128)(2,1)} %broadcast_in_dim.85), calls=%async_computation.2 | async-start | bytes 1048576 | tf_op jit(solution)/shard_map/all_to_all | solution.py:67
  81.1 2.8 collective-permute-done.4.refs_1_
  89.3 6.7 %all-to-all-done.2.refs_0_ = bf16[4,256,256]{2,1,0:T(8,128)(2,1)} async-done(((bf16[4,256,256]{2,1,0:T(8,128)(2,1)}), bf16[4,256,256]{2,1,0:T(8,128)(2,1)}, u32[]{:S(2)}, u32[]{:S(2)}) %all-to-all-start.2) | async-done | bytes 524320 | tf_op jit(solution)/shard_map/all_to_all | solution.py:67
  106.6 3.1 %collective-permute-done.14.refs_1_ = bf16[4,256,256]{2,1,0:T(8,128)(2,1)} collective-permute-done((bf16[4,256,256]{2,1,0:T(8,128)(2,1)}, bf16[4,256,256]{2,1,0:T(8,128)(2,1)}, u32[]{:S(2)}, u32[]{:S(2)}) %collective-permute-start.14) | collective-permute-done | bytes 524320 | tf_op jit(solution)/shard_map/ppermute | solution.py:54
  113.8 7.5 %collective-permute-done.16 = bf16[2,256,256]{2,1,0:T(8,128)(2,1)S(1)} collective-permute-done((bf16[2,256,256]{2,1,0:T(8,128)(2,1)S(1)}, bf16[2,256,256]{2,1,0:T(8,128)(2,1)S(1)}, u32[]{:S(2)}, u32[]{:S(2)}) %collective-permute-start.16) | collective-permute-done | bytes 262176 | tf_op jit(solution)/shard_map/ppermute | solution.py:54
  122.1 5.7 %collective-permute-done.17 = bf16[2,256,256]{2,1,0:T(8,128)(2,1)S(1)} collective-permute-done((bf16[2,256,256]{2,1,0:T(8,128)(2,1)S(1)}, bf16[2,256,256]{2,1,0:T(8,128)(2,1)S(1)}, u32[]{:S(2)}, u32[]{:S(2)}) %collective-permute-start.17) | collective-permute-done | bytes 262176 | tf_op jit(solution)/shard_map/ppermute | solution.py:54
  140.3 4.5 %collective-permute-start.22 = (bf16[512,256]{1,0:T(8,128)(2,1)}, bf16[512,256]{1,0:T(8,128)(2,1)}, u32[]{:S(2)}, u32[]{:S(2)}) collective-permute-start(bf16[512,256]{1,0:T(8,128)(2,1)} %param.19), channel_id=1, source_target_pairs={{0,0},{1,8},{2,16},{3,24},{4,32},{5,40},{6,48},{7,56},{8,1},{9,9},... | collective-permute-start | bytes 786440 | tf_op jit(solution)/shard_map/ppermute | solution.py:300
  151.3 6.0 %shard_map.109.query_ref = bf16[256,512]{1,0:T(8,128)(2,1)S(1)} custom-call(s32[79]{0:T(128)S(1)} %copy-done.9, bf16[256,8192]{1,0:T(8,128)(2,1)S(1)} %copy-done.1, f32[1,8192]{1,0:T(1,128)S(1)} %bitcast.32, f32[1,512]{1,0:T(1,128)S(1)} %bitcast.34, f32[256,128]{1,0:T(8,128)S(1)} %get-tuple-element.30.cos_ref, f32[256,128]{1,0:T(8,128)S(1)} %get-tuple-element.6.sin_ref, ...), custom_call_target="tpu_custom_call" | custom-call | flops 2147483648 | bytes 12582912 | tf_op jit(solution)/shard_map/pallas_call | solution.py:36
  157.4 4.1 %shard_map.111 = bf16[256,512]{1,0:T(8,128)(2,1)S(1)} custom-call(s32[79]{0:T(128)S(1)} %copy-done.9, bf16[256,512]{1,0:T(8,128)(2,1)S(1)} %shard_map.109.query_ref, s32[1,256]{1,0:T(1,128)S(1)} %bitcast.33, bf16[4,256,256]{2,1,0:T(8,128)(2,1)} %all-to-all-done.2.refs_0_, bf16[4,256,256]{2,1,0:T(8,128)(2,1)} %collective-permute-done.14.refs_1_, ...), custom_call_target="tpu_custom_call" | custom-call | flops 6442450944 | bytes 5242880 | tf_op jit(solution)/shard_map/pallas_call | solution.py:36
  163.0 4.6 %all-to-all-start.3 = ((bf16[8,256,512]{2,1,0:T(8,128)(2,1)}), bf16[8,256,512]{2,1,0:T(8,128)(2,1)S(1)}, u32[]{:S(2)}, u32[]{:S(2)}) async-start(bf16[8,256,512]{2,1,0:T(8,128)(2,1)} %broadcast_in_dim.86), calls=%async_computation.3 | async-start | bytes 4194304 | tf_op jit(solution)/shard_map/all_to_all | solution.py:67
  167.6 11.8 %collective-permute-start.24 = (bf16[512,256]{1,0:T(8,128)(2,1)}, bf16[512,256]{1,0:T(8,128)(2,1)S(1)}, u32[]{:S(2)}, u32[]{:S(2)}) collective-permute-start(bf16[512,256]{1,0:T(8,128)(2,1)} %collective-permute-done.22), channel_id=1, source_target_pairs={{0,192},{64,0},{128,64},{192,128},{1,193},{65,1},{129,65},{193,129... | collective-permute-start | bytes 786440 | tf_op jit(solution)/shard_map/ppermute | solution.py:54
  179.3 5.1 %collective-permute-done.24 = bf16[512,256]{1,0:T(8,128)(2,1)S(1)} collective-permute-done((bf16[512,256]{1,0:T(8,128)(2,1)}, bf16[512,256]{1,0:T(8,128)(2,1)S(1)}, u32[]{:S(2)}, u32[]{:S(2)}) %collective-permute-start.24) | collective-permute-done | bytes 262176 | tf_op jit(solution)/shard_map/ppermute | solution.py:54
  184.5 4.3 %collective-permute-start.26 = (bf16[256,256]{1,0:T(8,128)(2,1)S(1)}, bf16[256,256]{1,0:T(8,128)(2,1)S(1)}, u32[]{:S(2)}, u32[]{:S(2)}) collective-permute-start(bf16[256,256]{1,0:T(8,128)(2,1)S(1)} %slice.55), channel_id=1, source_target_pairs={{0,192},{64,0},{128,64},{192,128},{1,193},{65,1},{129,65},{193,129... | collective-permute-start | bytes 393224 | tf_op jit(solution)/shard_map/ppermute | solution.py:54
  188.7 24.9 %collective-permute-done.23 = bf16[512,256]{1,0:T(8,128)(2,1)S(1)} collective-permute-done((bf16[512,256]{1,0:T(8,128)(2,1)}, bf16[512,256]{1,0:T(8,128)(2,1)S(1)}, u32[]{:S(2)}, u32[]{:S(2)}) %collective-permute-start.23) | collective-permute-done | bytes 262176 | tf_op jit(solution)/shard_map/ppermute | solution.py:54
  213.7 5.9 %collective-permute-done.25 = bf16[256,256]{1,0:T(8,128)(2,1)S(1)} collective-permute-done((bf16[256,256]{1,0:T(8,128)(2,1)S(1)}, bf16[256,256]{1,0:T(8,128)(2,1)S(1)}, u32[]{:S(2)}, u32[]{:S(2)}) %collective-permute-start.25) | collective-permute-done | bytes 131104 | tf_op jit(solution)/shard_map/ppermute | solution.py:54
  223.5 20.6 %collective-permute-done.27.refs_1_ = bf16[4,512,256]{2,1,0:T(8,128)(2,1)S(1)} collective-permute-done((bf16[4,512,256]{2,1,0:T(8,128)(2,1)S(1)}, bf16[4,512,256]{2,1,0:T(8,128)(2,1)S(1)}, u32[]{:S(2)}, u32[]{:S(2)}) %collective-permute-start.27) | collective-permute-done | bytes 1048608 | tf_op jit(solution)/shard_map/ppermute | solution.py:54
  244.3 2.7 collective-permute-start.30
  247.0 4.1 %collective-permute-start.31 = (bf16[4,512,256]{2,1,0:T(8,128)(2,1)S(1)}, bf16[4,512,256]{2,1,0:T(8,128)(2,1)S(1)}, u32[]{:S(2)}, u32[]{:S(2)}) collective-permute-start(bf16[4,512,256]{2,1,0:T(8,128)(2,1)S(1)} %pad_maximum_fusion.1.refs_0_), channel_id=1, source_target_pairs={{0,8},{8,0},{1,9},{9,1},{2,10},{10,2},{3,11},{11,3},{4,12},{12,4},... | collective-permute-start | bytes 3145736 | tf_op jit(solution)/shard_map/ppermute | solution.py:58
  251.6 3.7 %collective-permute-done.29 = bf16[2,512,256]{2,1,0:T(8,128)(2,1)S(1)} collective-permute-done((bf16[2,512,256]{2,1,0:T(8,128)(2,1)S(1)}, bf16[2,512,256]{2,1,0:T(8,128)(2,1)S(1)}, u32[]{:S(2)}, u32[]{:S(2)}) %collective-permute-start.29) | collective-permute-done | bytes 524320 | tf_op jit(solution)/shard_map/ppermute | solution.py:54
  255.4 4.5 %collective-permute-start.34 = (bf16[4,512,256]{2,1,0:T(8,128)(2,1)S(1)}, bf16[4,512,256]{2,1,0:T(8,128)(2,1)}, u32[]{:S(2)}, u32[]{:S(2)}) collective-permute-start(bf16[4,512,256]{2,1,0:T(8,128)(2,1)S(1)} %constant_dynamic-update-slice_fusion.4.refs_3_), channel_id=1, source_target_pairs={{0,8},{8,0},{1,9},{9,1},{2,10},{10,2},{3,11},{11,3},{4,12},{12,4},... | collective-permute-start | bytes 3145736 | tf_op jit(solution)/shard_map/ppermute | solution.py:58
  263.7 7.2 %shard_map.112 = bf16[256,1024]{1,0:T(8,128)(2,1)} custom-call(s32[79]{0:T(128)S(1)} %copy-done.10, bf16[8,256,512]{2,1,0:T(8,128)(2,1)} %copy-done.11, bf16[4,512,256]{2,1,0:T(8,128)(2,1)} %copy-done.12, bf16[4,512,256]{2,1,0:T(8,128)(2,1)} %copy-done.13, bf16[4,512,256]{2,1,0:T(8,128)(2,1)} %copy-done.14, bf16[4,512,256]{2,1,0:T(8,128)(2,1)} %copy-done.15, ...), custom_call_target="tpu_custom_call" | custom-call | flops 2147483648 | bytes 12582912 | tf_op jit(solution)/shard_map/pallas_call | solution.py:36
  270.8 9.5 %all-to-all-start.4 = ((bf16[8,32,1024]{2,1,0:T(8,128)(2,1)}), bf16[8,32,1024]{2,1,0:T(8,128)(2,1)S(1)}, u32[]{:S(2)}, u32[]{:S(2)}) async-start(bf16[8,32,1024]{2,1,0:T(8,128)(2,1)} %bitcast.22), calls=%async_computation.4 | async-start | bytes 1048576 | tf_op jit(solution)/shard_map/all_to_all | solution.py:388
  281.5 8.2 %all-to-all-done.4.landed_ref = bf16[8,32,1024]{2,1,0:T(8,128)(2,1)S(1)} async-done(((bf16[8,32,1024]{2,1,0:T(8,128)(2,1)}), bf16[8,32,1024]{2,1,0:T(8,128)(2,1)S(1)}, u32[]{:S(2)}, u32[]{:S(2)}) %all-to-all-start.4) | async-done | bytes 524320 | tf_op jit(solution)/shard_map/all_to_all | solution.py:388
  (156 shorter events, 66.2 us)
Async XLA Ops:
  0.0 46.5 %collective-permute-start.1 = (bf16[256,512]{1,0:T(8,128)(2,1)}, bf16[256,512]{1,0:T(8,128)(2,1)S(1)}, u32[]{:S(2)}, u32[]{:S(2)}) collective-permute-start(bf16[256,512]{1,0:T(8,128)(2,1)} %param.13), channel_id=1, source_target_pairs={{0,192},{64,0},{128,64},{192,128},{1,193},{65,1},{129,65},{193,129... | collective-permute-start | bytes 786440 | tf_op jit(solution)/shard_map/ppermute | solution.py:54
  6.9 44.9 %collective-permute-start = (bf16[256,512]{1,0:T(8,128)(2,1)}, bf16[256,512]{1,0:T(8,128)(2,1)S(1)}, u32[]{:S(2)}, u32[]{:S(2)}) collective-permute-start(bf16[256,512]{1,0:T(8,128)(2,1)} %param.13), channel_id=1, source_target_pairs={{0,64},{64,128},{128,192},{192,0},{1,65},{65,129},{129,193},{193,1... | collective-permute-start | bytes 786440 | tf_op jit(solution)/shard_map/ppermute | solution.py:54
  8.6 14.2 %all-to-all-start = ((bf16[4,256,128]{2,1,0:T(8,128)(2,1)}), bf16[4,256,128]{2,1,0:T(8,128)(2,1)S(1)}, u32[]{:S(2)}, u32[]{:S(2)}) async-start(bf16[4,256,128]{2,1,0:T(8,128)(2,1)} %broadcast_in_dim.46), calls=%async_computation | async-start | bytes 524288 | tf_op jit(solution)/shard_map/all_to_all | solution.py:67
  24.0 13.8 %all-to-all-start.1 = ((bf16[4,4,256,128]{3,2,1,0:T(8,128)(2,1)}), bf16[4,4,256,128]{3,2,1,0:T(8,128)(2,1)S(1)}, u32[]{:S(2)}, u32[]{:S(2)}) async-start(bf16[4,4,256,128]{3,2,1,0:T(8,128)(2,1)} %broadcast_in_dim.84), calls=%async_computation.1 | async-start | bytes 2097152 | tf_op jit(solution)/shard_map/all_to_all | solution.py:67
  37.8 25.5 %collective-permute-start.12 = (bf16[16,256,128]{2,1,0:T(8,128)(2,1)S(1)}, bf16[16,256,128]{2,1,0:T(8,128)(2,1)}, u32[]{:S(2)}, u32[]{:S(2)}) collective-permute-start(bf16[16,256,128]{2,1,0:T(8,128)(2,1)S(1)} %bitcast.29), channel_id=1, source_target_pairs={{0,8},{8,0},{1,9},{9,1},{2,10},{10,2},{3,11},{11,3},{4,12},{12,4},... | collective-permute-start | bytes 3145736 | tf_op jit(solution)/shard_map/ppermute | solution.py:58
  46.5 11.9 %collective-permute-start.3 = (bf16[128,512]{1,0:T(8,128)(2,1)S(1)}, bf16[128,512]{1,0:T(8,128)(2,1)S(1)}, u32[]{:S(2)}, u32[]{:S(2)}) collective-permute-start(bf16[128,512]{1,0:T(8,128)(2,1)S(1)} %slice.49), channel_id=1, source_target_pairs={{0,192},{64,0},{128,64},{192,128},{1,193},{65,1},{129,65},{193,129... | collective-permute-start | bytes 393224 | tf_op jit(solution)/shard_map/ppermute | solution.py:54
  59.1 24.8 %collective-permute-start.4 = (bf16[4,256,512]{2,1,0:T(8,128)(2,1)S(1)}, bf16[4,256,512]{2,1,0:T(8,128)(2,1)S(1)}, u32[]{:S(2)}, u32[]{:S(2)}) collective-permute-start(bf16[4,256,512]{2,1,0:T(8,128)(2,1)S(1)} %pad_maximum_fusion.refs_0_), channel_id=1, source_target_pairs={{0,16},{16,32},{32,48},{48,0},{1,17},{17,33},{33,49},{49,1},{2,18}... | collective-permute-start | bytes 3145736 | tf_op jit(solution)/shard_map/ppermute | solution.py:54
  59.4 25.3 %collective-permute-start.5 = (bf16[4,256,512]{2,1,0:T(8,128)(2,1)S(1)}, bf16[4,256,512]{2,1,0:T(8,128)(2,1)}, u32[]{:S(2)}, u32[]{:S(2)}) collective-permute-start(bf16[4,256,512]{2,1,0:T(8,128)(2,1)S(1)} %pad_maximum_fusion.refs_0_), channel_id=1, source_target_pairs={{0,48},{16,0},{32,16},{48,32},{1,49},{17,1},{33,17},{49,33},{2,50}... | collective-permute-start | bytes 3145736 | tf_op jit(solution)/shard_map/ppermute | solution.py:54
  75.1 20.8 %all-to-all-start.2 = ((bf16[4,256,256]{2,1,0:T(8,128)(2,1)}), bf16[4,256,256]{2,1,0:T(8,128)(2,1)}, u32[]{:S(2)}, u32[]{:S(2)}) async-start(bf16[4,256,256]{2,1,0:T(8,128)(2,1)} %broadcast_in_dim.85), calls=%async_computation.2 | async-start | bytes 1048576 | tf_op jit(solution)/shard_map/all_to_all | solution.py:67
  84.7 15.8 %collective-permute-start.6 = (bf16[2,256,512]{2,1,0:T(8,128)(2,1)}, bf16[2,256,512]{2,1,0:T(8,128)(2,1)S(1)}, u32[]{:S(2)}, u32[]{:S(2)}) collective-permute-start(bf16[2,256,512]{2,1,0:T(8,128)(2,1)} %slice.50), channel_id=1, source_target_pairs={{0,16},{16,32},{32,48},{48,0},{1,17},{17,33},{33,49},{49,1},{2,18}... | collective-permute-start | bytes 1572872 | tf_op jit(solution)/shard_map/ppermute | solution.py:54
  86.6 14.0 %collective-permute-start.7 = (bf16[2,256,512]{2,1,0:T(8,128)(2,1)}, bf16[2,256,512]{2,1,0:T(8,128)(2,1)S(1)}, u32[]{:S(2)}, u32[]{:S(2)}) collective-permute-start(bf16[2,256,512]{2,1,0:T(8,128)(2,1)} %slice.51), channel_id=1, source_target_pairs={{0,48},{16,0},{32,16},{48,32},{1,49},{17,1},{33,17},{49,33},{2,50}... | collective-permute-start | bytes 1572872 | tf_op jit(solution)/shard_map/ppermute | solution.py:54
  95.9 13.7 %collective-permute-start.14 = (bf16[4,256,256]{2,1,0:T(8,128)(2,1)}, bf16[4,256,256]{2,1,0:T(8,128)(2,1)}, u32[]{:S(2)}, u32[]{:S(2)}) collective-permute-start(bf16[4,256,256]{2,1,0:T(8,128)(2,1)} %all-to-all-done.2.refs_0_), channel_id=1, source_target_pairs={{0,16},{16,32},{32,48},{48,0},{1,17},{17,33},{33,49},{49,1},{2,18}... | collective-permute-start | bytes 1572872 | tf_op jit(solution)/shard_map/ppermute | solution.py:54
  95.9 16.8 %collective-permute-start.15 = (bf16[4,256,256]{2,1,0:T(8,128)(2,1)}, bf16[4,256,256]{2,1,0:T(8,128)(2,1)}, u32[]{:S(2)}, u32[]{:S(2)}) collective-permute-start(bf16[4,256,256]{2,1,0:T(8,128)(2,1)} %all-to-all-done.2.refs_0_), channel_id=1, source_target_pairs={{0,48},{16,0},{32,16},{48,32},{1,49},{17,1},{33,17},{49,33},{2,50}... | collective-permute-start | bytes 1572872 | tf_op jit(solution)/shard_map/ppermute | solution.py:54
  98.6 32.2 %collective-permute-start.8 = (bf16[4,256,512]{2,1,0:T(8,128)(2,1)S(1)}, bf16[4,256,512]{2,1,0:T(8,128)(2,1)S(1)}, u32[]{:S(2)}, u32[]{:S(2)}) collective-permute-start(bf16[4,256,512]{2,1,0:T(8,128)(2,1)S(1)} %pad_maximum_fusion.refs_0_), channel_id=1, source_target_pairs={{0,8},{8,0},{1,9},{9,1},{2,10},{10,2},{3,11},{11,3},{4,12},{12,4},... | collective-permute-start | bytes 3145736 | tf_op jit(solution)/shard_map/ppermute | solution.py:58
  100.5 31.3 %collective-permute-start.9 = (bf16[4,256,512]{2,1,0:T(8,128)(2,1)S(1)}, bf16[4,256,512]{2,1,0:T(8,128)(2,1)S(1)}, u32[]{:S(2)}, u32[]{:S(2)}) collective-permute-start(bf16[4,256,512]{2,1,0:T(8,128)(2,1)S(1)} %collective-permute-done.4.refs_1_), channel_id=1, source_target_pairs={{0,8},{8,0},{1,9},{9,1},{2,10},{10,2},{3,11},{11,3},{4,12},{12,4},... | collective-permute-start | bytes 3145736 | tf_op jit(solution)/shard_map/ppermute | solution.py:58
  102.1 31.2 %collective-permute-start.10 = (bf16[4,256,512]{2,1,0:T(8,128)(2,1)}, bf16[4,256,512]{2,1,0:T(8,128)(2,1)S(1)}, u32[]{:S(2)}, u32[]{:S(2)}) collective-permute-start(bf16[4,256,512]{2,1,0:T(8,128)(2,1)} %collective-permute-done.5.refs_2_), channel_id=1, source_target_pairs={{0,8},{8,0},{1,9},{9,1},{2,10},{10,2},{3,11},{11,3},{4,12},{12,4},... | collective-permute-start | bytes 3145736 | tf_op jit(solution)/shard_map/ppermute | solution.py:58
  109.7 30.7 %collective-permute-start.11 = (bf16[4,256,512]{2,1,0:T(8,128)(2,1)S(1)}, bf16[4,256,512]{2,1,0:T(8,128)(2,1)}, u32[]{:S(2)}, u32[]{:S(2)}) collective-permute-start(bf16[4,256,512]{2,1,0:T(8,128)(2,1)S(1)} %constant_dynamic-update-slice_fusion.refs_3_), channel_id=1, source_target_pairs={{0,8},{8,0},{1,9},{9,1},{2,10},{10,2},{3,11},{11,3},{4,12},{12,4},... | collective-permute-start | bytes 3145736 | tf_op jit(solution)/shard_map/ppermute | solution.py:58
  127.8 29.5 %collective-permute-start.18 = (bf16[4,256,256]{2,1,0:T(8,128)(2,1)}, bf16[4,256,256]{2,1,0:T(8,128)(2,1)}, u32[]{:S(2)}, u32[]{:S(2)}) collective-permute-start(bf16[4,256,256]{2,1,0:T(8,128)(2,1)} %all-to-all-done.2.refs_0_), channel_id=1, source_target_pairs={{0,8},{8,0},{1,9},{9,1},{2,10},{10,2},{3,11},{11,3},{4,12},{12,4},... | collective-permute-start | bytes 1572872 | tf_op jit(solution)/shard_map/ppermute | solution.py:58
  131.8 25.6 %collective-permute-start.19 = (bf16[4,256,256]{2,1,0:T(8,128)(2,1)}, bf16[4,256,256]{2,1,0:T(8,128)(2,1)}, u32[]{:S(2)}, u32[]{:S(2)}) collective-permute-start(bf16[4,256,256]{2,1,0:T(8,128)(2,1)} %collective-permute-done.14.refs_1_), channel_id=1, source_target_pairs={{0,8},{8,0},{1,9},{9,1},{2,10},{10,2},{3,11},{11,3},{4,12},{12,4},... | collective-permute-start | bytes 1572872 | tf_op jit(solution)/shard_map/ppermute | solution.py:58
  132.8 24.6 %collective-permute-start.20 = (bf16[4,256,256]{2,1,0:T(8,128)(2,1)}, bf16[4,256,256]{2,1,0:T(8,128)(2,1)}, u32[]{:S(2)}, u32[]{:S(2)}) collective-permute-start(bf16[4,256,256]{2,1,0:T(8,128)(2,1)} %collective-permute-done.15.refs_2_), channel_id=1, source_target_pairs={{0,8},{8,0},{1,9},{9,1},{2,10},{10,2},{3,11},{11,3},{4,12},{12,4},... | collective-permute-start | bytes 1572872 | tf_op jit(solution)/shard_map/ppermute | solution.py:58
  134.3 23.1 %collective-permute-start.21 = (bf16[4,256,256]{2,1,0:T(8,128)(2,1)}, bf16[4,256,256]{2,1,0:T(8,128)(2,1)}, u32[]{:S(2)}, u32[]{:S(2)}) collective-permute-start(bf16[4,256,256]{2,1,0:T(8,128)(2,1)} %constant_dynamic-update-slice_fusion.2.refs_3_), channel_id=1, source_target_pairs={{0,8},{8,0},{1,9},{9,1},{2,10},{10,2},{3,11},{11,3},{4,12},{12,4},... | collective-permute-start | bytes 1572872 | tf_op jit(solution)/shard_map/ppermute | solution.py:58
  140.3 27.2 %collective-permute-start.22 = (bf16[512,256]{1,0:T(8,128)(2,1)}, bf16[512,256]{1,0:T(8,128)(2,1)}, u32[]{:S(2)}, u32[]{:S(2)}) collective-permute-start(bf16[512,256]{1,0:T(8,128)(2,1)} %param.19), channel_id=1, source_target_pairs={{0,0},{1,8},{2,16},{3,24},{4,32},{5,40},{6,48},{7,56},{8,1},{9,9},... | collective-permute-start | bytes 786440 | tf_op jit(solution)/shard_map/ppermute | solution.py:300
  163.0 99.4 %all-to-all-start.3 = ((bf16[8,256,512]{2,1,0:T(8,128)(2,1)}), bf16[8,256,512]{2,1,0:T(8,128)(2,1)S(1)}, u32[]{:S(2)}, u32[]{:S(2)}) async-start(bf16[8,256,512]{2,1,0:T(8,128)(2,1)} %broadcast_in_dim.86), calls=%async_computation.3 | async-start | bytes 4194304 | tf_op jit(solution)/shard_map/all_to_all | solution.py:67
  167.6 16.9 %collective-permute-start.24 = (bf16[512,256]{1,0:T(8,128)(2,1)}, bf16[512,256]{1,0:T(8,128)(2,1)S(1)}, u32[]{:S(2)}, u32[]{:S(2)}) collective-permute-start(bf16[512,256]{1,0:T(8,128)(2,1)} %collective-permute-done.22), channel_id=1, source_target_pairs={{0,192},{64,0},{128,64},{192,128},{1,193},{65,1},{129,65},{193,129... | collective-permute-start | bytes 786440 | tf_op jit(solution)/shard_map/ppermute | solution.py:54
  179.3 34.3 %collective-permute-start.23 = (bf16[512,256]{1,0:T(8,128)(2,1)}, bf16[512,256]{1,0:T(8,128)(2,1)S(1)}, u32[]{:S(2)}, u32[]{:S(2)}) collective-permute-start(bf16[512,256]{1,0:T(8,128)(2,1)} %collective-permute-done.22), channel_id=1, source_target_pairs={{0,64},{64,128},{128,192},{192,0},{1,65},{65,129},{129,193},{193,1... | collective-permute-start | bytes 786440 | tf_op jit(solution)/shard_map/ppermute | solution.py:54
  184.5 29.2 %collective-permute-start.26 = (bf16[256,256]{1,0:T(8,128)(2,1)S(1)}, bf16[256,256]{1,0:T(8,128)(2,1)S(1)}, u32[]{:S(2)}, u32[]{:S(2)}) collective-permute-start(bf16[256,256]{1,0:T(8,128)(2,1)S(1)} %slice.55), channel_id=1, source_target_pairs={{0,192},{64,0},{128,64},{192,128},{1,193},{65,1},{129,65},{193,129... | collective-permute-start | bytes 393224 | tf_op jit(solution)/shard_map/ppermute | solution.py:54
  220.7 23.3 %collective-permute-start.27 = (bf16[4,512,256]{2,1,0:T(8,128)(2,1)S(1)}, bf16[4,512,256]{2,1,0:T(8,128)(2,1)S(1)}, u32[]{:S(2)}, u32[]{:S(2)}) collective-permute-start(bf16[4,512,256]{2,1,0:T(8,128)(2,1)S(1)} %pad_maximum_fusion.1.refs_0_), channel_id=1, source_target_pairs={{0,16},{16,32},{32,48},{48,0},{1,17},{17,33},{33,49},{49,1},{2,18}... | collective-permute-start | bytes 3145736 | tf_op jit(solution)/shard_map/ppermute | solution.py:54
  220.8 23.4 %collective-permute-start.28 = (bf16[4,512,256]{2,1,0:T(8,128)(2,1)S(1)}, bf16[4,512,256]{2,1,0:T(8,128)(2,1)S(1)}, u32[]{:S(2)}, u32[]{:S(2)}) collective-permute-start(bf16[4,512,256]{2,1,0:T(8,128)(2,1)S(1)} %pad_maximum_fusion.1.refs_0_), channel_id=1, source_target_pairs={{0,48},{16,0},{32,16},{48,32},{1,49},{17,1},{33,17},{49,33},{2,50}... | collective-permute-start | bytes 3145736 | tf_op jit(solution)/shard_map/ppermute | solution.py:54
  244.1 11.2 %collective-permute-start.29 = (bf16[2,512,256]{2,1,0:T(8,128)(2,1)S(1)}, bf16[2,512,256]{2,1,0:T(8,128)(2,1)S(1)}, u32[]{:S(2)}, u32[]{:S(2)}) collective-permute-start(bf16[2,512,256]{2,1,0:T(8,128)(2,1)S(1)} %slice.56), channel_id=1, source_target_pairs={{0,16},{16,32},{32,48},{48,0},{1,17},{17,33},{33,49},{49,1},{2,18}... | collective-permute-start | bytes 1572872 | tf_op jit(solution)/shard_map/ppermute | solution.py:54
  244.3 11.1 %collective-permute-start.30 = (bf16[2,512,256]{2,1,0:T(8,128)(2,1)S(1)}, bf16[2,512,256]{2,1,0:T(8,128)(2,1)S(1)}, u32[]{:S(2)}, u32[]{:S(2)}) collective-permute-start(bf16[2,512,256]{2,1,0:T(8,128)(2,1)S(1)} %slice.57), channel_id=1, source_target_pairs={{0,48},{16,0},{32,16},{48,32},{1,49},{17,1},{33,17},{49,33},{2,50}... | collective-permute-start | bytes 1572872 | tf_op jit(solution)/shard_map/ppermute | solution.py:54
  247.0 12.9 %collective-permute-start.31 = (bf16[4,512,256]{2,1,0:T(8,128)(2,1)S(1)}, bf16[4,512,256]{2,1,0:T(8,128)(2,1)S(1)}, u32[]{:S(2)}, u32[]{:S(2)}) collective-permute-start(bf16[4,512,256]{2,1,0:T(8,128)(2,1)S(1)} %pad_maximum_fusion.1.refs_0_), channel_id=1, source_target_pairs={{0,8},{8,0},{1,9},{9,1},{2,10},{10,2},{3,11},{11,3},{4,12},{12,4},... | collective-permute-start | bytes 3145736 | tf_op jit(solution)/shard_map/ppermute | solution.py:58
  270.8 18.8 %all-to-all-start.4 = ((bf16[8,32,1024]{2,1,0:T(8,128)(2,1)}), bf16[8,32,1024]{2,1,0:T(8,128)(2,1)S(1)}, u32[]{:S(2)}, u32[]{:S(2)}) async-start(bf16[8,32,1024]{2,1,0:T(8,128)(2,1)} %bitcast.22), calls=%async_computation.4 | async-start | bytes 1048576 | tf_op jit(solution)/shard_map/all_to_all | solution.py:388
  (34 other events, 580.0 us)
